TPU v7x, 8 devices: a whole 2x2x1 slice. The times are simulated.
8 devices in a mesh: rep: 1 (over z), r: 2 (over y), s: 4 (over x, core).
Axes of the slice: x: 2, y: 2, z: 1, core: 2. Of those that a mesh axis runs over, the one named last changes fastest.
Arguments:
- x: bfloat16 [8, 4096, 768], P(('rep', 'r', 's'))
- dy: bfloat16 [8, 4096, 768], P(('rep', 'r', 's'))
- w_gate: bfloat16 [2, 768, 6144], P(None, 's')
- w_up: bfloat16 [2, 768, 6144], P(None, 's')
- w_down: bfloat16 [2, 6144, 768], P(None, 's')
Outputs:
- output 1: bfloat16 [8, 4096, 768], P(('rep', 'r', 's'))
- output 2: bfloat16 [2, 768, 6144], P('rep', 's')
- output 3: bfloat16 [2, 768, 6144], P('rep', 's')
- output 4: bfloat16 [2, 6144, 768], P('rep', 's')
All inputs are finite; a program needn't handle non-finite values.
Results may differ from a plain program's by a relative error of at most 0.018.
Values are sent between devices in bfloat16 or wider.
A program may use at most 2 GiB of HBM per device.

v0:
```python
import jax
import jax.numpy as jnp
from jax import lax
from jax.sharding import PartitionSpec as P

NAMES = ("w_gate", "w_up", "w_down")


def matmul(a, w):
    return jnp.dot(a, w, preferred_element_type=jnp.float32).astype(jnp.bfloat16)


def normed(h):
    wide = h.astype(jnp.float32)
    scale = lax.rsqrt(jnp.mean(wide**2, -1, keepdims=True) + 1e-6)
    return (wide * scale).astype(jnp.bfloat16)


def layer(h, w):
    a = normed(h)
    gate = jnp.dot(a, w["w_gate"], preferred_element_type=jnp.float32)
    up = jnp.dot(a, w["w_up"], preferred_element_type=jnp.float32)
    return h + matmul((jax.nn.silu(gate) * up).astype(jnp.bfloat16), w["w_down"])


def solution(mesh):
    def fetched(weights, number):
        return {name: lax.all_gather(w[number], "s", axis=0, tiled=True) for name, w in zip(NAMES, weights, strict=True)}

    def summed(term):
        return lax.psum(lax.psum_scatter(term, "s", scatter_dimension=0, tiled=True), "r")

    def step(x, dy, *weights):
        layers = weights[0].shape[0]
        h, inputs = x[0], []
        for number in range(layers):
            inputs.append(h)
            h = layer(h, fetched(weights, number))
        by_h, mine = dy[0], [None] * layers
        for number in reversed(range(layers)):
            _, back = jax.vjp(lambda w, h: layer(h, w), fetched(weights, number), inputs[number])
            by_w, by_h = back(by_h)
            mine[number] = [summed(by_w[name]) for name in NAMES]
        return (by_h[None], *(jnp.stack([mine[number][i] for number in range(layers)]) for i in range(3)))

    states, cut = P(("rep", "r", "s"), None, None), P(None, "s", None)
    return jax.shard_map(
        step,
        mesh=mesh,
        in_specs=(states, states) + (cut,) * 3,
        out_specs=(states,) + (P("rep", "s", None),) * 3,
        check_vma=False,
    )
```

profile of v0, /device:TPU:0, one launch (start us, length us, event | category | flops | bytes accessed | tf_op | source)
XLA Modules:
  0.0 1577.4 jit_solution(2486252300294422040)
XLA Ops:
  7.2 0.0 all-gather.13.cloned.1.call-start
  7.2 5.1 fusion.87
  12.3 0.0 all-gather.13.cloned.1.call-update
  12.3 0.0 all-gather.15.cloned.1.call-start
  12.4 5.1 fusion.86
  17.5 0.0 all-gather.15.cloned.1.call-update
  17.5 0.0 all-gather.17.cloned.1.call-start
  17.6 4.8 fusion.85
  22.3 0.0 all-gather.17.cloned.1.call-update
  22.4 0.0 all-gather.21.cloned.1.call-start
  22.4 0.5 all-gather.21.cloned.1.call-update
  22.9 0.0 all-gather.23.cloned.1.call-start
  23.0 0.5 all-gather.23.cloned.1.call-update
  23.5 0.0 all-gather.19.cloned.1.call-start
  23.6 0.5 all-gather.19.cloned.1.call-update
  24.1 0.0 reduce-scatter.15.cloned.1.call-start
  24.2 8.6 copy.10
  32.8 4.1 fusion.15
  36.9 0.6 copy-done.1
  37.5 8.8 copy.9
  46.2 30.9 %all-gather.13.cloned.1.call-done = bf16[1,768,6144]{2,1,0:T(8,128)(2,1)} async-done(((bf16[1,192,6144]{2,1,0:T(8,128)(2,1)}), bf16[1,768,6144]{2,1,0:T(8,128)(2,1)}) %all-gather.13.cloned.1.call-update) | async-done | bytes 9437200 | tf_op jit(solution)/shard_map/all_gather | solution.py:28
  77.1 49.9 %fusion.40 = f32[4096,6144]{1,0:T(8,128)} fusion(bf16[1,768,6144]{2,1,0:T(8,128)(2,1)} %all-gather.13.cloned.1.call-done, bf16[1,4096,768]{1,2,0:T(8,128)(2,1)} %copy.10, f32[4096]{0:T(1024)S(1)} %fusion.78), kind=kOutput, calls=%fused_computation.65 | convolution fusion | flops 38664142848 | bytes 116408320 | tf_op jit(solution)/shard_map/dot_general | solution.py:21
  127.0 13.4 all-gather.15.cloned.1.call-done
  140.4 96.9 %multiply_convert_fusion.1 = (bf16[4096,6144]{1,0:T(8,128)(2,1)}, f32[4096,6144]{1,0:T(8,128)}) fusion(f32[4096,6144]{1,0:T(8,128)} %fusion.40, bf16[1,768,6144]{2,1,0:T(8,128)(2,1)} %all-gather.15.cloned.1.call-done, bf16[1,4096,768]{1,2,0:T(8,128)(2,1)} %copy.10, f32[4096]{0:T(1024)S(1)} %fusion.78), kind=kOutput, calls=%fused_computation.13 | convolution fusion | flops 38815137792 | bytes 267403264 | tf_op jit(solution)/shard_map/dot_general | solution.py:22
  237.3 47.9 %fusion.18 = (f32[4096]{0:T(1024)S(1)}, bf16[4096,768]{0,1:T(8,128)(2,1)}) fusion(bf16[4096,6144]{1,0:T(8,128)(2,1)} %get-tuple-element.20, bf16[1,6144,768]{2,1,0:T(8,128)(2,1)} %all-gather.17.cloned.1.call-done, bf16[1,4096,768]{1,2,0:T(8,128)(2,1)} %copy.10), kind=kOutput, calls=%fused_computation.40 | convolution fusion | flops 38670430208 | bytes 72368128 | tf_op jit(solution)/shard_map/dot_general | solution.py:10
  285.2 47.4 %convolution_convert_fusion.1 = bf16[4096,6144]{1,0:T(8,128)(2,1)} fusion(bf16[1,6144,768]{2,1,0:T(8,128)(2,1)} %all-gather.21.cloned.1.call-done, bf16[1,4096,768]{2,1,0:T(8,128)(2,1)} %param.6), kind=kOutput, calls=%fused_computation.22 | convolution fusion | flops 38679871488 | bytes 66060288 | tf_op jit(solution)/shard_map/transpose(jvp())/dot_general | solution.py:10
  332.6 0.0 all-gather.23.cloned.1.call-done
  332.7 49.9 %fusion.24 = f32[4096,6144]{1,0:T(8,128)} fusion(bf16[1,768,6144]{2,1,0:T(8,128)(2,1)} %all-gather.23.cloned.1.call-done, bf16[4096,768]{0,1:T(8,128)(2,1)} %get-tuple-element.23, f32[4096]{0:T(1024)S(1)} %fusion.79), kind=kOutput, calls=%fused_computation.49 | convolution fusion | flops 38664142848 | bytes 116408320 | tf_op jit(solution)/shard_map/jvp()/dot_general | solution.py:22
  382.6 11.9 all-gather.19.cloned.1.call-done
  394.5 125.5 %fusion.1 = (bf16[4096,6144]{1,0:T(8,128)(2,1)}, f32[4096,6144]{1,0:T(8,128)}) fusion(f32[4096,6144]{1,0:T(8,128)} %fusion.24, bf16[4096,6144]{1,0:T(8,128)(2,1)} %convolution_convert_fusion.1, bf16[1,768,6144]{2,1,0:T(8,128)(2,1)} %all-gather.19.cloned.1.call-done, bf16[4096,768]{0,1:T(8,128)(2,1)} %get-tuple-element.23, f32[4096]{0:T(1024)S(1)} %fusion.79), kind=kOutput, calls=%fused_computation.7 | convolution fusion | flops 38966132736 | bytes 317734912 | tf_op jit(solution)/shard_map/jvp()/dot_general | solution.py:21
  520.0 47.0 %fusion.48 = bf16[4096,768]{0,1:T(8,128)(2,1)} fusion(bf16[4096,6144]{1,0:T(8,128)(2,1)} %get-tuple-element.24, bf16[1,768,6144]{2,1,0:T(8,128)(2,1)} %all-gather.19.cloned.1.call-done), kind=kOutput, calls=%fused_computation.69 | convolution fusion | flops 38654705664 | bytes 66060288 | tf_op jit(solution)/shard_map/transpose(jvp())/dot_general | solution.py:21
  567.0 68.1 %fusion.20 = (f32[4096]{0:T(1024)S(1)}, bf16[4096,768]{0,1:T(8,128)(2,1)}) fusion(bf16[4096,768]{0,1:T(8,128)(2,1)} %get-tuple-element.23, bf16[4096,768]{0,1:T(8,128)(2,1)} %fusion.48, bf16[1,768,6144]{2,1,0:T(8,128)(2,1)} %all-gather.23.cloned.1.call-done, bf16[4096,6144]{1,0:T(8,128)(2,1)} %convolution_convert_fusion.1, f32[4096,6144]{1,0:T(8,128)} %get-tuple-element.25), kind=kOutput, calls=%fused_computation.42 | convolution fusion | flops 38824570880 | bytes 179322880 | tf_op jit(solution)/shard_map/transpose(jvp())/dot_general | solution.py:22
  635.1 8.2 fusion.59
  643.4 2.6 copy-done
  646.0 45.4 %convolution_convert_fusion.2 = bf16[6144,768]{1,0:T(8,128)(2,1)} fusion(bf16[4096,6144]{1,0:T(8,128)(2,1)} %get-tuple-element.20, bf16[4096,768]{0,1:T(8,128)(2,1)S(1)} %fusion.59), kind=kOutput, calls=%fused_computation.46 | convolution fusion | flops 38659424256 | bytes 66060288 | tf_op jit(solution)/shard_map/transpose(jvp())/dot_general | solution.py:10
  691.4 0.0 reduce-scatter.15.cloned.1.call-update
  691.4 0.0 reduce-scatter.17.cloned.1.call-start
  691.5 70.5 %fusion.21 = bf16[6144,768]{1,0:T(8,128)(2,1)} fusion(f32[4096,6144]{1,0:T(8,128)} %fusion.24, bf16[1,4096,768]{2,1,0:T(8,128)(2,1)} %param.6, f32[4096,6144]{1,0:T(8,128)} %get-tuple-element.25), kind=kOutput, calls=%fused_computation.43 | convolution fusion | flops 38810419200 | bytes 217055232 | tf_op jit(solution)/shard_map/transpose(jvp())/dot_general | solution.py:10
  762.0 0.0 reduce-scatter.17.cloned.1.call-update
  762.0 0.0 reduce-scatter.11.cloned.1.call-start
  762.1 123.1 %fusion.3 = (bf16[4096,6144]{1,0:T(8,128)(2,1)}, bf16[4096,6144]{1,0:T(8,128)(2,1)}) fusion(f32[4096,6144]{1,0:T(8,128)} %fusion.40, f32[4096,6144]{1,0:T(8,128)} %get-tuple-element.21, bf16[4096,768]{0,1:T(8,128)(2,1)} %copy-done, bf16[1,6144,768]{2,1,0:T(8,128)(2,1)} %all-gather.17.cloned.1.call-done), kind=kOutput, calls=%fused_computation.9 | convolution fusion | flops 38981861376 | bytes 317718528 | tf_op jit(solution)/shard_map/transpose(jvp())/dot_general | solution.py:10
  885.2 59.2 %fusion.22 = bf16[768,6144]{1,0:T(8,128)(2,1)} fusion(bf16[4096,6144]{1,0:T(8,128)(2,1)} %get-tuple-element.29, bf16[1,4096,768]{1,2,0:T(8,128)(2,1)} %copy.10, f32[4096]{0:T(1024)S(1)} %copy-done.4, f32[4096,6144]{1,0:T(8,128)} %fusion.40), kind=kOutput, calls=%fused_computation.44 | convolution fusion | flops 38819856384 | bytes 166739968 | tf_op jit(solution)/shard_map/transpose(jvp())/dot_general | solution.py:22
  944.4 0.0 reduce-scatter.11.cloned.1.call-update
  944.4 0.0 reduce-scatter.13.cloned.1.call-start
  944.5 59.5 %fusion.23 = bf16[768,6144]{1,0:T(8,128)(2,1)} fusion(bf16[4096,6144]{1,0:T(8,128)(2,1)} %convolution_convert_fusion.1, bf16[4096,768]{0,1:T(8,128)(2,1)} %get-tuple-element.23, f32[4096]{0:T(1024)S(1)} %copy-done.9, f32[4096,6144]{1,0:T(8,128)} %get-tuple-element.25), kind=kOutput, calls=%fused_computation.45 | convolution fusion | flops 38819856384 | bytes 166739968 | tf_op jit(solution)/shard_map/transpose(jvp())/dot_general | solution.py:22
  1004.0 0.0 reduce-scatter.13.cloned.1.call-update
  1004.1 0.0 reduce-scatter.9.cloned.1.call-start
  1004.1 46.4 %convolution_convert_fusion.3 = bf16[768,6144]{1,0:T(8,128)(2,1)} fusion(bf16[4096,6144]{1,0:T(8,128)(2,1)} %get-tuple-element.24, bf16[4096,768]{0,1:T(8,128)(2,1)} %get-tuple-element.23, f32[4096]{0:T(1024)S(1)} %copy-done.9), kind=kOutput, calls=%fused_computation.47 | convolution fusion | flops 38664142848 | bytes 66076672 | tf_op jit(solution)/shard_map/transpose(jvp())/dot_general | solution.py:21
  1050.5 0.0 reduce-scatter.9.cloned.1.call-update
  1050.5 0.0 reduce-scatter.7.cloned.1.call-start
  1050.6 46.3 %convolution_convert_fusion.4 = bf16[768,6144]{1,0:T(8,128)(2,1)} fusion(bf16[4096,6144]{1,0:T(8,128)(2,1)} %get-tuple-element.28, bf16[1,4096,768]{1,2,0:T(8,128)(2,1)} %copy.10, f32[4096]{0:T(1024)S(1)} %copy-done.5), kind=kOutput, calls=%fused_computation.48 | convolution fusion | flops 38664142848 | bytes 66076672 | tf_op jit(solution)/shard_map/transpose(jvp())/dot_general | solution.py:21
  1096.9 0.0 reduce-scatter.7.cloned.1.call-update
  1096.9 0.0 all-reduce.3.cloned.1.call-start
  1097.0 47.2 %fusion.42 = bf16[4096,768]{0,1:T(8,128)(2,1)} fusion(bf16[4096,6144]{1,0:T(8,128)(2,1)} %get-tuple-element.28, bf16[1,768,6144]{2,1,0:T(8,128)(2,1)} %all-gather.13.cloned.1.call-done), kind=kOutput, calls=%fused_computation.67 | convolution fusion | flops 38654705664 | bytes 66060288 | tf_op jit(solution)/shard_map/transpose(jvp())/dot_general | solution.py:21
  1144.2 0.0 reduce-scatter.13.cloned.1.call-done
  1144.2 19.9 %reduce-scatter.9.cloned.1.call-done = bf16[192,6144]{1,0:T(8,128)(2,1)} async-done(((bf16[768,6144]{1,0:T(8,128)(2,1)}), bf16[192,6144]{1,0:T(8,128)(2,1)}) %reduce-scatter.9.cloned.1.call-update) | async-done | bytes 2359312 | tf_op jit(solution)/shard_map/reduce_scatter | solution.py:31
  1164.2 74.0 %reduce-scatter.7.cloned.1.call-done = bf16[192,6144]{1,0:T(8,128)(2,1)} async-done(((bf16[768,6144]{1,0:T(8,128)(2,1)}), bf16[192,6144]{1,0:T(8,128)(2,1)}) %reduce-scatter.7.cloned.1.call-update) | async-done | bytes 2359312 | tf_op jit(solution)/shard_map/reduce_scatter | solution.py:31
  1238.2 0.0 all-reduce.3.cloned.1.call-update
  1238.2 67.8 %fusion.17 = (f32[4096]{0:T(1024)S(1)}, bf16[4096,768]{0,1:T(8,128)(2,1)}) fusion(bf16[1,4096,768]{1,2,0:T(8,128)(2,1)} %copy.10, bf16[4096,768]{0,1:T(8,128)(2,1)} %fusion.42, bf16[1,768,6144]{2,1,0:T(8,128)(2,1)} %all-gather.15.cloned.1.call-done, bf16[4096,6144]{1,0:T(8,128)(2,1)} %get-tuple-element.29, f32[4096,6144]{1,0:T(8,128)} %fusion.40), kind=kOutput, calls=%fused_computation.39 | convolution fusion | flops 38824570880 | bytes 179322880 | tf_op jit(solution)/shard_map/transpose(jvp())/dot_general | solution.py:22
  1306.1 11.1 fusion.58
  1317.2 8.6 copy.11
  1325.8 231.4 %all-reduce.3.cloned.1.call-done = (bf16[1,192,6144]{2,1,0:T(8,128)(2,1)}, bf16[1,192,6144]{2,1,0:T(8,128)(2,1)}, bf16[1,192,6144]{2,1,0:T(8,128)(2,1)}, bf16[1,...) async-done(((bf16[1,192,6144]{2,1,0:T(8,128)(2,1)}, bf16[1,192,6144]{2,1,0:T(8,128)(2,1)}, bf16[1,192,6144]{2,1,0:T(8,128)(2,1)}, ...) | async-done | bytes 14155792 | tf_op jit(solution)/shard_map/psum | solution.py:31
  1557.2 5.0 pad_maximum_fusion.2
  1562.2 8.3 pad_maximum_fusion
  (31 shorter events, 0.1 us)
Async XLA Ops:
  7.2 69.9 %all-gather.13.cloned.1.call-start = ((), (), s32[]{:S(2)}) async-start(), calls=%async_computation.12 | async-start | bytes 11796480 | tf_op jit(solution)/shard_map/all_gather | solution.py:28
  12.3 128.1 %all-gather.15.cloned.1.call-start = ((), (), s32[]{:S(2)}) async-start(), calls=%async_computation.13 | async-start | bytes 11796480 | tf_op jit(solution)/shard_map/all_gather | solution.py:28
  17.5 219.8 %all-gather.17.cloned.1.call-start = ((), (), s32[]{:S(2)}) async-start(), calls=%async_computation.14 | async-start | bytes 11796480 | tf_op jit(solution)/shard_map/all_gather | solution.py:28
  22.4 262.8 %all-gather.21.cloned.1.call-start = ((), (), s32[]{:S(2)}) async-start(), calls=%async_computation.16 | async-start | bytes 11796480 | tf_op jit(solution)/shard_map/all_gather | solution.py:28
  22.9 309.7 %all-gather.23.cloned.1.call-start = ((), (), s32[]{:S(2)}) async-start(), calls=%async_computation.17 | async-start | bytes 11796480 | tf_op jit(solution)/shard_map/all_gather | solution.py:28
  23.5 371.0 %all-gather.19.cloned.1.call-start = ((), (), s32[]{:S(2)}) async-start(), calls=%async_computation.15 | async-start | bytes 11796480 | tf_op jit(solution)/shard_map/all_gather | solution.py:28
  24.1 1120.1 %reduce-scatter.15.cloned.1.call-start = ((), (), s32[]{:S(2)}) async-start(), calls=%async_computation.10 | async-start | bytes 11796480 | tf_op jit(solution)/shard_map/reduce_scatter | solution.py:31
  36.9 0.6 copy-start.1
  37.5 103.0 %copy-start.3 = (f32[4096]{0:T(1024)}, f32[4096]{0:T(1024)S(1)}, u32[]{:S(2)}) copy-start(f32[4096]{0:T(1024)S(1)} %fusion.78) | copy-start | bytes 49156
  285.2 47.4 %copy-start.10 = (f32[4096]{0:T(1024)}, f32[4096]{0:T(1024)S(1)}, u32[]{:S(2)}) copy-start(f32[4096]{0:T(1024)S(1)} %get-tuple-element.22) | copy-start | bytes 49156
  332.6 61.9 %copy-start.7 = (f32[4096]{0:T(1024)}, f32[4096]{0:T(1024)S(1)}, u32[]{:S(2)}) copy-start(f32[4096]{0:T(1024)S(1)} %fusion.79) | copy-start | bytes 49156
  567.0 68.1 %copy-start.11 = (f32[4096]{0:T(1024)S(1)}, f32[4096]{0:T(1024)}, u32[]{:S(2)}) copy-start(f32[4096]{0:T(1024)} %copy-done.10) | copy-start | bytes 49156
  567.0 68.2 %copy-start.8 = (f32[4096]{0:T(1024)S(1)}, f32[4096]{0:T(1024)}, u32[]{:S(2)}) copy-start(f32[4096]{0:T(1024)} %copy-done.7) | copy-start | bytes 49156
  643.4 2.6 copy-start
  691.4 452.8 %reduce-scatter.17.cloned.1.call-start = ((), (), s32[]{:S(2)}) async-start(), calls=%async_computation.11 | async-start | bytes 11796480 | tf_op jit(solution)/shard_map/reduce_scatter | solution.py:31
  762.0 382.2 %reduce-scatter.11.cloned.1.call-start = ((), (), s32[]{:S(2)}) async-start(), calls=%async_computation.8 | async-start | bytes 11796480 | tf_op jit(solution)/shard_map/reduce_scatter | solution.py:31
  762.1 123.1 %copy-start.4 = (f32[4096]{0:T(1024)S(1)}, f32[4096]{0:T(1024)}, u32[]{:S(2)}) copy-start(f32[4096]{0:T(1024)} %copy-done.3) | copy-start | bytes 49156
  885.2 59.3 %copy-start.9 = (f32[4096]{0:T(1024)S(1)}, f32[4096]{0:T(1024)}, u32[]{:S(2)}) copy-start(f32[4096]{0:T(1024)} %copy-done.7) | copy-start | bytes 49156
  944.4 199.8 %reduce-scatter.13.cloned.1.call-start = ((), (), s32[]{:S(2)}) async-start(), calls=%async_computation.9 | async-start | bytes 11796480 | tf_op jit(solution)/shard_map/reduce_scatter | solution.py:31
  1004.0 46.5 %copy-start.5 = (f32[4096]{0:T(1024)S(1)}, f32[4096]{0:T(1024)}, u32[]{:S(2)}) copy-start(f32[4096]{0:T(1024)} %copy-done.3) | copy-start | bytes 49156
  1004.1 160.1 %reduce-scatter.9.cloned.1.call-start = ((), (), s32[]{:S(2)}) async-start(), calls=%async_computation.7 | async-start | bytes 11796480 | tf_op jit(solution)/shard_map/reduce_scatter | solution.py:31
  1050.5 187.7 %reduce-scatter.7.cloned.1.call-start = ((), (), s32[]{:S(2)}) async-start(), calls=%async_computation.6 | async-start | bytes 11796480 | tf_op jit(solution)/shard_map/reduce_scatter | solution.py:31
  1096.9 460.2 %all-reduce.3.cloned.1.call-start = ((), (), s32[]{:S(2)}) async-start(), calls=%async_computation.18 | async-start | bytes 28311552 | tf_op jit(solution)/shard_map/psum | solution.py:31
  1238.2 67.9 %copy-start.2 = (f32[4096]{0:T(1024)S(1)}, f32[4096]{0:T(1024)}, u32[]{:S(2)}) copy-start(f32[4096]{0:T(1024)} %copy-done.1) | copy-start | bytes 49156
  1238.2 67.9 %copy-start.6 = (f32[4096]{0:T(1024)S(1)}, f32[4096]{0:T(1024)}, u32[]{:S(2)}) copy-start(f32[4096]{0:T(1024)} %copy-done.3) | copy-start | bytes 49156
Sparse Core Ops, SparseCore 0:
  12.4 64.5 all-gather.12
  78.6 61.7 all-gather.14
  142.0 61.7 all-gather.16
  205.1 61.7 all-gather.20
  268.9 61.7 all-gather.22
  332.7 61.7 all-gather.18
  691.5 71.5 reduce-scatter.14
  765.7 71.5 reduce-scatter.16
  944.5 71.5 reduce-scatter.10
  1018.5 71.5 reduce-scatter.12
  1092.6 71.5 reduce-scatter.8
  1166.6 71.5 reduce-scatter.6
  1241.1 316.0 all-reduce.2
where the time goes:
time: 1590 us; the launch traced here: 1580 us
  matrix products  1100 us (69%)
  waiting for transfers between devices  383 us (24%)
  local copies, waits for them, and re-layouts  44.2 us (3%)
  other arithmetic  36.8 us (2%)
    dot_general x6, matrix products, layer(): up = jnp.dot(a, w['w_up'], preferred_element_type=jnp.float32)  402 us
    dot_general x6, matrix products, layer(): gate = jnp.dot(a, w['w_gate'], preferred_element_type=jnp.float32)  362 us
    dot_general x5, matrix products, matmul(): jnp.dot(a, w, preferred_element_type=jnp.float32).astype(jnp.bfloat16)  334 us
    psum x1, waiting for transfers between devices, summed(): lax.psum(lax.psum_scatter(term, 's', scatter_dimension=0, tiled=True), 'r')  231 us
    reduce_scatter x6, waiting for transfers between devices, summed(): lax.psum_scatter(term, 's', scatter_dimension=0, tiled=True)  93.9 us
    all_gather x6, waiting for transfers between devices, fetched(): lax.all_gather(w[number], 's', axis=0, tiled=True)  56.2 us
  transfers between devices with their start and end apart: 13, of which 6 were waited for; matrix products, arithmetic and copies ran while one was open for 55% of the time, Pallas kernels for 0%

commit v1 on v0

v1 whole, which is shorter than its diff:
```python
import functools

import jax
import jax.numpy as jnp
from jax import lax
from jax.experimental import pallas as pl
from jax.experimental.pallas import tpu as pltpu
from jax.sharding import PartitionSpec as P

f32, bf16 = jnp.float32, jnp.bfloat16
TOK, D, FF, L = 4096, 768, 6144, 2
S = 4
C = 512
J = FF // C
W = C // S
RD, RF = D // S, FF // S
PR = 2 * RD + W * D // C
VM = 67043328
once = pl.Buffered(1)


def dot(a, b, ca=1, cb=0):
    return lax.dot_general(a, b, (((ca,), (cb,)), ((), ())), preferred_element_type=f32)


def normed(wide):
    scale = lax.rsqrt(jnp.mean(wide**2, -1, keepdims=True) + 1e-6)
    return wide * scale, scale


def gate_of(w):
    return jnp.concatenate([w[s, 0:RD, :] for s in range(S)], axis=0)


def up_of(w):
    return jnp.concatenate([w[s, RD : 2 * RD, :] for s in range(S)], axis=0)


def down_of(w, at=2 * RD):
    def rows(s):
        fold = jnp.concatenate([w[s, at + W : at + W + W // 2, 0 : D - C], w[s, at + W : at + W + W // 2, D - C : 2 * (D - C)]], axis=0)
        return jnp.concatenate([w[s, at : at + W, :], fold], axis=1)

    return jnp.concatenate([rows(s) for s in range(S)], axis=0)


def piece_slices(j):
    for s in range(S):
        cols = pl.ds(pl.multiple_of(RF * s + W * j, W), W)
        yield 0, (pl.ds(0, RD), cols), (pl.ds(0, RD), pl.ds(W * s, W))
        yield 1, (pl.ds(0, RD), cols), (pl.ds(RD, RD), pl.ds(W * s, W))
    at = pl.multiple_of(W * j, W)
    yield 2, (pl.ds(at, W), pl.ds(0, C)), (pl.ds(2 * RD, W), pl.ds(0, C))
    yield 2, (pl.ds(at, W // 2), pl.ds(C, D - C)), (pl.ds(2 * RD + W, W // 2), pl.ds(0, D - C))
    yield 2, (pl.ds(at + W // 2, W // 2), pl.ds(C, D - C)), (pl.ds(2 * RD + W, W // 2), pl.ds(D - C, D - C))


def prep_kernel(x, wg, wu, wd, a, at, whole, stage, sems):
    i = pl.program_id(0)
    me = lax.axis_index("s")
    n = pl.num_programs(0)
    per = L * J // 8
    slot = lax.rem(i, 2)
    for q in range(per):
        k = i * per + q
        l, j = k // J, lax.rem(k, J)
        for m, src, dst in piece_slices(j):
            pltpu.make_async_copy((wg, wu, wd)[m].at[(l, *src)], stage.at[(slot, q, *dst)], sems.at[0, q]).start()
    y, _ = normed(x[...].astype(f32))
    y = y.astype(bf16)
    a[...] = y
    at[...] = y.T
    for q in range(per):
        k = i * per + q
        l, j = k // J, lax.rem(k, J)
        pltpu.make_async_copy(whole.at[l, me, j], stage.at[slot, q], sems.at[0, q]).wait()

        @pl.when(i > 0)
        def _():
            pltpu.make_async_copy(stage.at[1 - slot, q], whole.at[l, me, j], sems.at[1, q]).wait()

        out = pltpu.make_async_copy(stage.at[slot, q], whole.at[l, me, j], sems.at[1, q])
        out.start()

        @pl.when(i == n - 1)
        def _():
            out.wait()


def prep(x, wg, wu, wd):
    T = TOK // 8
    hbm = pl.BlockSpec(memory_space=pl.ANY)
    return pl.pallas_call(
        prep_kernel,
        grid=(8,),
        in_specs=[pl.BlockSpec((T, D), lambda i: (i, 0)), hbm, hbm, hbm],
        out_specs=[pl.BlockSpec((T, D), lambda i: (i, 0)), pl.BlockSpec((D, T), lambda i: (0, i)), hbm],
        out_shape=[jax.ShapeDtypeStruct((TOK, D), bf16), jax.ShapeDtypeStruct((D, TOK), bf16), jax.ShapeDtypeStruct((L, S, J, PR, C), bf16)],
        scratch_shapes=[pltpu.VMEM((2, L * J // 8, PR, C), bf16), pltpu.SemaphoreType.DMA((2, L * J // 8))],
        compiler_params=pltpu.CompilerParams(vmem_limit_bytes=VM),
        name="prep",
    )(x, wg, wu, wd)


MESH = pl.DeviceIdType.MESH
HALF = PR // 2
hbm = pl.BlockSpec(memory_space=pl.ANY)


def place():
    me, y = lax.axis_index("s"), lax.axis_index("r")
    return me, y, {"s": me + 1 - 2 * lax.rem(me, 2)}, {"s": lax.rem(me + 2, S)}, {"r": 1 - y}


def greet():
    _, _, core, across, copy = place()
    barrier = pltpu.get_barrier_semaphore()
    for to in (core, across, copy):
        pl.semaphore_signal(barrier, inc=1, device_id=to, device_id_type=MESH)
    pl.semaphore_wait(barrier, 3)


def remote(src, dst, send, recv, to):
    return pltpu.make_async_remote_copy(src_ref=src, dst_ref=dst, send_sem=send, recv_sem=recv, device_id=to, device_id_type=MESH)


class Gather:
    def __init__(self, whole, send, recv, first):
        self.whole, self.send, self.recv, self.first = whole, send, recv, first

    def copy(self, k, n):
        me, y, core, across, copy = place()
        l, j = k // J, lax.rem(k, J)
        near, far = pl.ds(pl.multiple_of(HALF * y, HALF), HALF), pl.ds(pl.multiple_of(HALF * (1 - y), HALF), HALF)
        s = me if n < 2 else lax.rem(me + 2, S)
        what = self.whole.at[(l, s, j, *((), (near,), (near,), (near,), (far,))[n])]
        return remote(what, what, self.send.at[lax.rem(k, 8), n], self.recv.at[k - self.first, n], (core, across, copy, core, core)[n])

    def start(self, k):
        self.copy(k, 0).start()
        self.copy(k, 1).start()

    def across(self, k):
        self.copy(k, 1).wait_recv()
        self.copy(k, 2).start()
        self.copy(k, 3).start()

    def along(self, k):
        self.copy(k, 2).wait_recv()
        self.copy(k, 4).start()

    def finish(self, k):
        for n in (0, 3, 4):
            self.copy(k, n).wait_recv()
        for n in range(5):
            self.copy(k, n).wait_send()


def fetch(whole, held, sem, l, j):
    slot = lax.rem(j, 2)
    return [pltpu.make_async_copy(whole.at[l, s, j], held.at[slot, s], sem.at[slot, s]) for s in range(S)]


AHEAD = 5
EARLY = 2


def forward_kernel(a, x, _, h, a1, a1t, gs, us, whole, acc, held, send, recv, load):
    j, t = pl.program_id(0), pl.program_id(1)
    T = h.shape[0]
    gather = Gather(whole, send, recv, 0)
    K = J + EARLY

    @pl.when((j == 0) & (t == 0))
    def _():
        greet()
        for k in range(AHEAD):
            gather.start(k)
        gather.across(0)
        gather.across(1)
        gather.along(0)
        gather.finish(0)
        for copy in fetch(whole, held, load, 0, 0):
            copy.start()

    @pl.when(t == 0)
    def _():
        for copy in fetch(whole, held, load, 0, j):
            copy.wait()

        @pl.when(j + AHEAD < K)
        def _():
            gather.start(j + AHEAD)

    @pl.when((t == 1) & (j + 2 < K))
    def _():
        gather.across(j + 2)

    @pl.when(t == 2)
    def _():
        gather.along(j + 1)

    @pl.when(t == 3)
    def _():
        gather.finish(j + 1)

        @pl.when(j + 1 < J)
        def _():
            for copy in fetch(whole, held, load, 0, j + 1):
                copy.start()

    rows = pl.ds(pl.multiple_of(t * T, T), T)
    w = held.at[lax.rem(j, 2)]
    lhs = a[rows, :]
    g, u = dot(lhs, gate_of(w)), dot(lhs, up_of(w))
    gs[0], us[0] = g, u
    act = (g * jax.nn.sigmoid(g) * u).astype(bf16)
    acc[rows, :] = jnp.where(j == 0, 0.0, acc[rows, :]) + dot(act, down_of(w))

    @pl.when(j == J - 1)
    def _():
        out = x[...].astype(f32) + acc[rows, :].astype(bf16).astype(f32)
        out = out.astype(bf16)
        h[...] = out
        y, _ = normed(out.astype(f32))
        y = y.astype(bf16)
        a1[...] = y
        a1t[...] = y.T

    @pl.when((j == J - 1) & (t == pl.num_programs(1) - 1))
    def _():
        gather.along(J + 1)
        gather.finish(J + 1)


def forward(a, x, whole):
    T = 1024
    last = lambda j, t: (jnp.where(j == J - 1, t, 0), 0)
    lastT = lambda j, t: (0, jnp.where(j == J - 1, t, 0))
    return pl.pallas_call(
        forward_kernel,
        grid=(J, TOK // T),
        in_specs=[pl.BlockSpec((TOK, D), lambda j, t: (0, 0), pipeline_mode=once), pl.BlockSpec((T, D), last), hbm],
        out_specs=[pl.BlockSpec((T, D), last)] * 2 + [pl.BlockSpec((D, T), lastT)] + [pl.BlockSpec((1, T, C), lambda j, t: (j, t, 0))] * 2 + [hbm],
        out_shape=[jax.ShapeDtypeStruct((TOK, D), bf16)] * 2
        + [jax.ShapeDtypeStruct((D, TOK), bf16)]
        + [jax.ShapeDtypeStruct((J, TOK, C), f32)] * 2
        + [jax.ShapeDtypeStruct((L, S, J, PR, C), bf16)],
        scratch_shapes=[
            pltpu.VMEM((TOK, D), f32),
            pltpu.VMEM((2, S, PR, C), bf16),
            pltpu.SemaphoreType.DMA((8, 5)),
            pltpu.SemaphoreType.DMA((J + EARLY, 5)),
            pltpu.SemaphoreType.DMA((2, S)),
        ],
        input_output_aliases={2: 5},
        compiler_params=pltpu.CompilerParams(vmem_limit_bytes=VM, collective_id=0, has_side_effects=True),
        cost_estimate=pl.CostEstimate(flops=6 * TOK * D * FF, bytes_accessed=250 << 20, transcendentals=0),
        name="forward",
    )(a, x, whole)


def pack(s, ag, au, ad):
    rows = pl.ds(pl.multiple_of(RD * s, RD), RD)
    down = ad[:, pl.ds(pl.multiple_of(W * s, W), W)].T
    yield slice(0, RD), slice(0, C), ag[rows, :]
    yield slice(RD, 2 * RD), slice(0, C), au[rows, :]
    yield slice(2 * RD, 2 * RD + W), slice(0, C), down[:, :C]
    yield slice(2 * RD + W, PR), slice(0, D - C), down[: W // 2, C:]
    yield slice(2 * RD + W, PR), slice(D - C, C), down[W // 2 :, C:]


class Reduce:
    def __init__(self, sums, theirs, kept, out_a, in_a, kept_b, out_b, in_b, out_c, sa, sb, sc):
        self.sums, self.theirs = sums, theirs
        self.kept, self.out_a, self.in_a = kept, out_a, in_a
        self.kept_b, self.out_b, self.in_b, self.out_c = kept_b, out_b, in_b, out_c
        self.sa, self.sb, self.sc = sa, sb, sc

    def copy_a(self, j):
        slot = lax.rem(j, 2)
        return remote(self.out_a, self.in_a.at[slot], self.sa.at[0, 0], self.sa.at[1, slot], place()[2])

    def copy_b(self, j):
        slot = lax.rem(j, 2)
        return remote(self.out_b, self.in_b.at[slot], self.sb.at[0, 0], self.sb.at[1, slot], place()[3])

    def copy_c(self, j):
        slot = lax.rem(j, 2)
        return remote(self.out_c, self.theirs.at[j], self.sc.at[0, 0], self.sc.at[1, slot], place()[4])

    def store_c(self, j):
        return pltpu.make_async_copy(self.out_c, self.sums.at[j], self.sc.at[0, 1])

    def collect(self, ag, au, ad):
        c = lax.rem(lax.axis_index("s"), 2)
        for x in range(2):
            for r, cols, v in pack(2 * x + c, ag, au, ad):
                self.kept[x, r, cols] = v
            for r, cols, v in pack(2 * x + 1 - c, ag, au, ad):
                self.out_a[x, r, cols] = v.astype(bf16)

    def add_a(self, j):
        slot = lax.rem(j, 2)
        x = lax.axis_index("s") // 2
        self.kept_b[...] = self.kept[x] + self.in_a[slot, x].astype(f32)
        self.out_b[...] = (self.kept[1 - x] + self.in_a[slot, 1 - x].astype(f32)).astype(bf16)

    def add_b(self, j):
        self.out_c[...] = (self.kept_b[...] + self.in_b[lax.rem(j, 2)].astype(f32)).astype(bf16)


REDUCE_SCRATCH = [
    pltpu.VMEM((2, PR, C), f32),
    pltpu.VMEM((2, PR, C), bf16),
    pltpu.VMEM((2, 2, PR, C), bf16),
    pltpu.VMEM((PR, C), f32),
    pltpu.VMEM((PR, C), bf16),
    pltpu.VMEM((2, PR, C), bf16),
    pltpu.VMEM((PR, C), bf16),
    pltpu.SemaphoreType.DMA((2, 2)),
    pltpu.SemaphoreType.DMA((2, 2)),
    pltpu.SemaphoreType.DMA((2, 2)),
]


def weights_kernel(saved, *refs):
    if saved:
        at, dy, dyt, w, gs, us, sums, theirs, kept_o, out_o, dgs, dus, ag, au, ad, save, *rest = refs
    else:
        a, at, dy, dyt, _, sums, theirs, kept_o, out_o, dgs, dus, whole, ag, au, ad, save, held, send, recv, load, *rest = refs
        gather = Gather(whole, send, recv, J)
    reduce = Reduce(sums, theirs, *rest)
    j, t = pl.program_id(0), pl.program_id(1)
    T = dgs.shape[1]

    @pl.when((j == 0) & (t == 0))
    def _():
        greet()
        if not saved:
            gather.start(J + EARLY)
            for copy in fetch(whole, held, load, 1, 0):
                copy.start()

    if not saved:

        @pl.when(t == 0)
        def _():
            for copy in fetch(whole, held, load, 1, j):
                copy.wait()

            @pl.when(j + EARLY + 1 < J)
            def _():
                gather.start(J + j + EARLY + 1)

        @pl.when((t == 2) & (j + 2 >= EARLY) & (j + 2 < J))
        def _():
            gather.across(J + j + 2)

        @pl.when((t == 1) & (j + 1 >= EARLY) & (j + 1 < J))
        def _():
            gather.along(J + j + 1)

        @pl.when((t == 3) & (j + 1 < J))
        def _():
            @pl.when(j + 1 >= EARLY)
            def _():
                gather.finish(J + j + 1)

            for copy in fetch(whole, held, load, 1, j + 1):
                copy.start()

    @pl.when(t == 1)
    def _():
        @pl.when(j >= 3)
        def _():
            reduce.copy_c(j - 3).wait()
            reduce.store_c(j - 3).wait()

        @pl.when(j >= 2)
        def _():
            reduce.copy_b(j - 2).wait()
            reduce.add_b(j - 2)
            reduce.copy_c(j - 2).start()
            reduce.store_c(j - 2).start()

        @pl.when(j >= 1)
        def _():
            reduce.copy_a(j - 1).wait()
            reduce.add_a(j - 1)
            reduce.copy_b(j - 1).start()

    rows = pl.ds(pl.multiple_of(t * T, T), T)
    if saved:
        g, u = gs[0], us[0]
        down = down_of(w.at[0, :, 0], 0)
    else:
        w = held.at[lax.rem(j, 2)]
        lhs = a[rows, :]
        g, u = dot(lhs, gate_of(w)), dot(lhs, up_of(w))
        down = down_of(w)
    by = dot(dy[rows, :], down, 1, 1).astype(bf16).astype(f32)
    sig = jax.nn.sigmoid(g)
    silu = g * sig
    act = (silu * u).astype(bf16)
    du = (by * silu).astype(bf16)
    dg = (by * u * (sig + silu * (1 - sig))).astype(bf16)
    dgs[0], dus[0] = dg, du
    for acc, l, r in ((ag, at, dg), (au, at, du), (ad, dyt, act)):
        acc[...] = jnp.where(t == 0, 0.0, acc[...]) + dot(l[:, rows], r)

    @pl.when(t == pl.num_programs(1) - 1)
    def _():
        reduce.collect(ag, au, ad)

        @pl.when(j < J - 1)
        def _():
            reduce.copy_a(j).start()

        @pl.when(j == J - 1)
        def _():
            handed = [pltpu.make_async_copy(reduce.kept, kept_o, save.at[0]), pltpu.make_async_copy(reduce.out_a, out_o, save.at[1])]
            for copy in handed:
                copy.start()
            reduce.copy_c(J - 3).wait()
            reduce.store_c(J - 3).wait()
            reduce.copy_b(J - 2).wait()
            reduce.add_b(J - 2)
            reduce.store_c(J - 2).start()
            reduce.store_c(J - 2).wait()
            for copy in handed:
                copy.wait()


def weights_pass(saved, a, at, dy, dyt, whole, gs=None, us=None):
    T = 1024
    full = lambda shape: pl.BlockSpec(shape, lambda j, t: (0, 0), pipeline_mode=once)
    tile = pl.BlockSpec((1, T, C), lambda j, t: (j, t, 0))
    outs = [hbm] * 4 + [tile, tile]
    shapes = [
        jax.ShapeDtypeStruct((J, PR, C), bf16),
        jax.ShapeDtypeStruct((J, PR, C), bf16),
        jax.ShapeDtypeStruct((2, PR, C), f32),
        jax.ShapeDtypeStruct((2, PR, C), bf16),
    ] + [jax.ShapeDtypeStruct((J, TOK, C), bf16)] * 2
    scratch = [pltpu.VMEM((D, C), f32)] * 3 + [pltpu.SemaphoreType.DMA((2,))]
    if saved:
        ins = [full((D, TOK)), full((TOK, D)), full((D, TOK)), pl.BlockSpec((1, S, 1, PR - 2 * RD, C), lambda j, t: (0, 0, j, 2, 0)), tile, tile]
        args = (at, dy, dyt, whole, gs, us)
        alias = {}
    else:
        ins = [full((TOK, D)), full((D, TOK)), full((TOK, D)), full((D, TOK)), hbm]
        args = (a, at, dy, dyt, whole)
        outs.append(hbm)
        shapes.append(jax.ShapeDtypeStruct((L, S, J, PR, C), bf16))
        alias = {4: 6}
        scratch += [
            pltpu.VMEM((2, S, PR, C), bf16),
            pltpu.SemaphoreType.DMA((8, 5)),
            pltpu.SemaphoreType.DMA((J, 5)),
            pltpu.SemaphoreType.DMA((2, S)),
        ]
    return pl.pallas_call(
        functools.partial(weights_kernel, saved),
        grid=(J, TOK // T),
        in_specs=ins,
        out_specs=outs,
        out_shape=shapes,
        scratch_shapes=scratch + REDUCE_SCRATCH,
        input_output_aliases=alias,
        compiler_params=pltpu.CompilerParams(vmem_limit_bytes=VM, collective_id=2 if saved else 1, has_side_effects=True),
        cost_estimate=pl.CostEstimate(flops=(8 if saved else 12) * TOK * D * FF, bytes_accessed=300 << 20, transcendentals=0),
        name="weights_saved" if saved else "weights_again",
    )(*args)


def norm_back(by, h, dy):
    wide = h.astype(f32)
    scale = lax.rsqrt(jnp.mean(wide**2, -1, keepdims=True) + 1e-6)
    dot_ = jnp.sum(by * wide, -1, keepdims=True) / D
    by_h = (by * scale - wide * (scale * scale * scale * dot_)).astype(bf16)
    return (dy.astype(f32) + by_h.astype(f32)).astype(bf16)


Q = 2


def contract(j, dgs, dus, w, acc):
    total = jnp.where(j == 0, 0.0, acc[...])
    for q in range(Q):
        total = total + dot(dgs[q], gate_of(w.at[0, :, q]), 1, 1)
        total = total + dot(dus[q], up_of(w.at[0, :, q]), 1, 1)
    acc[...] = total


def input_kernel(transpose, dgs, dus, w, h, dy, sums_i, theirs_i, kept_i, out_i, *refs):
    if transpose:
        out, outt, sums, theirs, acc, load, *rest = refs
    else:
        out, sums, theirs, acc, load, *rest = refs
    reduce = Reduce(sums, theirs, *rest)
    t, j = pl.program_id(0), pl.program_id(1)
    step = t * pl.num_programs(1) + j
    second = lambda: remote(sums.at[J - 2], theirs.at[J - 2], load.at[1], load.at[2], place()[4])
    first = lambda: remote(out_i, reduce.in_a.at[1], reduce.sa.at[0, 0], reduce.sa.at[1, 1], place()[2])
    kept = lambda: pltpu.make_async_copy(kept_i, reduce.kept, load.at[0])

    @pl.when(step == 0)
    def _():
        greet()
        first().start()
        second().start()
        kept().start()

    @pl.when(step == 1)
    def _():
        first().wait()
        kept().wait()
        reduce.add_a(J - 1)
        reduce.copy_b(J - 1).start()

    @pl.when(step == 6)
    def _():
        reduce.copy_b(J - 1).wait()
        reduce.add_b(J - 1)
        reduce.copy_c(J - 1).start()
        reduce.store_c(J - 1).start()

    @pl.when(step == 11)
    def _():
        second().wait()
        reduce.copy_c(J - 1).wait()
        reduce.store_c(J - 1).wait()

    contract(j, dgs, dus, w, acc)

    @pl.when(j == pl.num_programs(1) - 1)
    def _():
        by = norm_back(acc[...].astype(bf16).astype(f32), h[...], dy[...])
        out[...] = by
        if transpose:
            outt[...] = by.T


def input_pass(l, dgs, dus, whole, h, dy, sums, theirs, kept, out_a):
    T = 1024
    n = TOK if l else TOK // 2
    tile = pl.BlockSpec((Q, T, C), lambda t, j: (j, t, 0))
    row = pl.BlockSpec((T, D), lambda t, j: (t, 0))
    return pl.pallas_call(
        functools.partial(input_kernel, l == 1),
        grid=(n // T, J // Q),
        in_specs=[tile, tile, pl.BlockSpec((1, S, Q, 2 * RD, C), lambda t, j: (l, 0, j, 0, 0)), row, row] + [hbm] * 4,
        out_specs=([row, pl.BlockSpec((D, T), lambda t, j: (0, t))] if l else [row]) + [hbm] * 2,
        out_shape=([jax.ShapeDtypeStruct((TOK, D), bf16), jax.ShapeDtypeStruct((D, TOK), bf16)] if l else [jax.ShapeDtypeStruct((n, D), bf16)])
        + [jax.ShapeDtypeStruct((J, PR, C), bf16)] * 2,
        scratch_shapes=[pltpu.VMEM((T, D), f32), pltpu.SemaphoreType.DMA((3,))] + REDUCE_SCRATCH,
        input_output_aliases={5: 2, 6: 3} if l else {5: 1, 6: 2},
        compiler_params=pltpu.CompilerParams(vmem_limit_bytes=VM, collective_id=3 + l, has_side_effects=True),
        cost_estimate=pl.CostEstimate(flops=4 * n * D * FF, bytes_accessed=150 << 20, transcendentals=0),
        name="input_pass",
    )(dgs, dus, whole, h, dy, sums, theirs, kept, out_a)


def last_kernel(dgs, dus, w, h, dy, begun, s1, t1, s0, t0, out, og, ou, od, acc, stage, sems):
    t, j = pl.program_id(0), pl.program_id(1)
    i = t * pl.num_programs(1) + j
    slot = lax.rem(i, 2)

    def copies(l):
        for m, dst, src in piece_slices(i):
            yield pltpu.make_async_copy(stage.at[(slot, l, *src)], (og, ou, od)[m].at[(l, *dst)], sems.at[slot, l])

    def wait(slot):
        for l in range(L):
            pltpu.make_async_copy(stage.at[slot, l], stage.at[slot, l], sems.at[slot, l]).wait()

    @pl.when(i >= 2)
    def _():
        wait(slot)

    for l, (mine, other) in enumerate(((s0, t0), (s1, t1))):
        stage[slot, l] = (mine[0].astype(f32) + other[0].astype(f32)).astype(bf16)
    contract(j, dgs, dus, w, acc)
    for l in range(L):
        for copy in copies(l):
            copy.start()

    @pl.when(j == pl.num_programs(1) - 1)
    def _():
        out[0] = begun[...]
        out[1] = norm_back(acc[...].astype(bf16).astype(f32), h[...], dy[...])

    @pl.when(i == J - 1)
    def _():
        wait(slot)
        wait(1 - slot)


def last_pass(dgs, dus, whole, h, dy, begun, s1, t1, s0, t0):
    T = 1024
    n = TOK // 2 // T
    steps = J // Q
    assert n * steps == J
    tile = pl.BlockSpec((Q, T, C), lambda t, j: (j, t + n, 0))
    row = pl.BlockSpec((T, D), lambda t, j: (t + n, 0))
    piece = pl.BlockSpec((1, PR, C), lambda t, j: (t * steps + j, 0, 0))
    return pl.pallas_call(
        last_kernel,
        grid=(n, steps),
        in_specs=[tile, tile, pl.BlockSpec((1, S, Q, 2 * RD, C), lambda t, j: (0, 0, j, 0, 0)), row, row, pl.BlockSpec((T, D), lambda t, j: (t, 0))]
        + [piece] * 4,
        out_specs=[pl.BlockSpec((2, T, D), lambda t, j: (0, t, 0))] + [hbm] * 3,
        out_shape=[jax.ShapeDtypeStruct((2, TOK // 2, D), bf16)] + [jax.ShapeDtypeStruct((L, RD, FF), bf16)] * 2 + [jax.ShapeDtypeStruct((L, RF, D), bf16)],
        scratch_shapes=[pltpu.VMEM((T, D), f32), pltpu.VMEM((2, L, PR, C), bf16), pltpu.SemaphoreType.DMA((2, L))],
        compiler_params=pltpu.CompilerParams(vmem_limit_bytes=VM),
        cost_estimate=pl.CostEstimate(flops=2 * TOK * D * FF, bytes_accessed=150 << 20, transcendentals=0),
        name="last_pass",
    )(dgs, dus, whole, h, dy, begun, s1, t1, s0, t0)


def transposed_kernel(x, y):
    y[...] = x[...].T


def transposed(x):
    T = 512
    return pl.pallas_call(
        transposed_kernel,
        grid=(TOK // T,),
        in_specs=[pl.BlockSpec((T, D), lambda i: (i, 0))],
        out_specs=pl.BlockSpec((D, T), lambda i: (0, i)),
        out_shape=jax.ShapeDtypeStruct((D, TOK), bf16),
        name="transposed",
    )(x)


def solution(mesh):
    def step(x, dy, wg, wu, wd):
        x, dy = x[0], dy[0]
        a0, a0t, whole = prep(x, wg, wu, wd)
        dyt = transposed(dy)
        h1, a1, a1t, gs, us, whole = forward(a0, x, whole)
        sums1, theirs1, kept, out_a, dgs, dus, whole = weights_pass(False, a1, a1t, dy, dyt, whole)
        by1, by1t, sums1, theirs1 = input_pass(1, dgs, dus, whole, h1, dy, sums1, theirs1, kept, out_a)
        sums0, theirs0, kept, out_a, dgs, dus = weights_pass(True, None, a0t, by1, by1t, whole, gs, us)
        begun, sums0, theirs0 = input_pass(0, dgs, dus, whole, x, by1, sums0, theirs0, kept, out_a)
        by0, *grads = last_pass(dgs, dus, whole, x, by1, begun, sums1, theirs1, sums0, theirs0)
        return (by0.reshape(1, TOK, D), *grads)

    states, cut = P(("rep", "r", "s"), None, None), P(None, "s", None)
    return jax.shard_map(
        step,
        mesh=mesh,
        in_specs=(states, states) + (cut,) * 3,
        out_specs=(states,) + (P("rep", "s", None),) * 3,
        check_vma=False,
    )
```

time: 1590 us -> 930 us (0.58)
  matrix products: 1100 us -> 0 us
  Pallas kernels: 0 us -> 928 us
  waiting for transfers between devices: 383 us -> 0 us
  local copies, waits for them, and re-layouts: 44.2 us -> 0 us
  other arithmetic: 36.8 us -> 0 us
    dot_general x17 -> x0, matrix products: 1100 us -> none  [the longest x6 402 us: layer(): up = jnp.dot(a, w['w_up'], preferred_element_type=jnp.float32)]
    pallas_call x0 -> x8, Pallas kernels: none -> 928 us  [the longest x2 503 us: weights_pass(): pl.pallas_call(functools.partial(weights_kernel, saved), grid=(J, TOK //...]
    psum x1 -> x0, waiting for transfers between devices: 231 us -> none  [summed(): lax.psum(lax.psum_scatter(term, 's', scatter_dimension=0, tiled=True), 'r')]
    reduce_scatter x6 -> x0, waiting for transfers between devices: 93.9 us -> none  [summed(): lax.psum_scatter(term, 's', scatter_dimension=0, tiled=True)]
    all_gather x6 -> x0, waiting for transfers between devices: 56.2 us -> none  [fetched(): lax.all_gather(w[number], 's', axis=0, tiled=True)]
    unnamed x27 -> x0, local copies, waits for them, and re-layouts: 29.2 us -> none
  transfers between devices with their start and end apart: 13 -> 0, of which waited for: 6 -> 0; matrix products, arithmetic and copies ran while one was open for 55% -> 0% of each run, Pallas kernels for 0% -> 0%
where the time goes in v1:
time: 930 us; the launch traced here: 929 us
  Pallas kernels  928 us (100%)
    pallas_call x2, Pallas kernels, weights_pass(): pl.pallas_call(functools.partial(weights_kernel, saved), grid=(J, TOK //...  503 us
    pallas_call x1, Pallas kernels, forward(): pl.pallas_call(forward_kernel, grid=(J, TOK // T), in_specs=[pl.BlockSpec...  177 us
    pallas_call x2, Pallas kernels, input_pass(): pl.pallas_call(functools.partial(input_kernel, l == 1), grid=(n // T, J /...  155 us
    pallas_call x1, Pallas kernels, last_pass(): pl.pallas_call(last_kernel, grid=(n, steps), in_specs=[tile, tile, pl.Blo...  60.9 us
    pallas_call x1, Pallas kernels, prep(): pl.pallas_call(prep_kernel, grid=(8,), in_specs=[pl.BlockSpec((T, D), lam...  23.4 us

profile of v1, /device:TPU:0, one launch (start us, length us, event | category | flops | bytes accessed | tf_op | source)
XLA Modules:
  0.0 929.0 jit_solution(5757695470161235055)
XLA Ops:
  0.6 8.6 transposed.1.refs_3_
  9.2 23.4 %prep.1 = (bf16[4096,768]{1,0:T(8,128)(2,1)}, bf16[768,4096]{1,0:T(8,128)(2,1)}, bf16[2,4,12,576,512]{4,3,2,1,0:T(8,128)(2,1)}) custom-call(bf16[4096,768]{1,0:T(8,128)(2,1)} %bitcast.3, bf16[2,192,6144]{2,1,0:T(8,128)(2,1)} %wg.1, bf16[2,192,6144]{2,1,0:T(8,128)(2,1)} %wu.1, bf16[2,1536,768]{2,1,0:T(8,128)(2,1)} %wd.1), custom_call_target="tpu_custom_call" | custom-call | tf_op jit(solution)/shard_map/prep/pallas_call | solution.py:93
  32.6 177.2 %forward.1 = (bf16[4096,768]{1,0:T(8,128)(2,1)}, bf16[4096,768]{1,0:T(8,128)(2,1)}, bf16[768,4096]{1,0:T(8,128)(2,1)}, f32[12,4096,512]{2,1,0:T(8,128)}, f32[12,...) custom-call(bf16[4096,768]{1,0:T(8,128)(2,1)} %get-tuple-element.38.a, ...), custom_call_target="tpu_custom_call", output_to_operand_aliasing={{5}: (2, {})} | custom-call | flops 115964116992 | bytes 262144000 | tf_op jit(solution)/shard_map/forward/pallas_call | solution.py:240
  209.8 295.4 %weights_again.1 = (bf16[12,576,512]{2,1,0:T(8,128)(2,1)}, bf16[12,576,512]{2,1,0:T(8,128)(2,1)}, f32[2,576,512]{2,1,0:T(8,128)}, bf16[2,576,512]{2,1,0:T(8,128)...) custom-call(bf16[4096,768]{1,0:T(8,128)(2,1)} %get-tuple-element.40., ...), custom_call_target="tpu_custom_call", output_to_operand_aliasing={{6}: (4, {})} | custom-call | flops 231928233984 | bytes 314572800 | tf_op jit(solution)/shard_map/weights_again/pallas_call | solution.py:463
  505.3 102.1 %input_pass.2 = (bf16[4096,768]{1,0:T(8,128)(2,1)}, bf16[768,4096]{1,0:T(8,128)(2,1)}, bf16[12,576,512]{2,1,0:T(8,128)(2,1)}, bf16[12,576,512]{2,1,0:T(8,128)(2,1)}) custom-call(bf16[12,4096,512]{2,1,0:T(8,128)(2,1)} %get-tuple-element.43.dgs, bf16[12,4096,512]{2,1,0:T(8,128)(2,1)} %get-tuple-element.44.dus, ...), custom_call_target="tpu_custom_call", output_to_operand_aliasing={{2}: (5, {}), {3}: (6, {})} | custom-call | flops 77309411328 | bytes 157286400 | tf_op jit(solution)/shard_map/input_pass/pallas_call | solution.py:550
  607.4 207.5 %weights_saved.1 = (bf16[12,576,512]{2,1,0:T(8,128)(2,1)}, bf16[12,576,512]{2,1,0:T(8,128)(2,1)}, f32[2,576,512]{2,1,0:T(8,128)}, bf16[2,576,512]{2,1,0:T(8,128)...) custom-call(bf16[768,4096]{1,0:T(8,128)(2,1)} %get-tuple-element.37.refs_0_, ...), custom_call_target="tpu_custom_call" | custom-call | flops 154618822656 | bytes 314572800 | tf_op jit(solution)/shard_map/weights_saved/pallas_call | solution.py:463
  815.0 52.9 %input_pass.3 = (bf16[2048,768]{1,0:T(8,128)(2,1)}, bf16[12,576,512]{2,1,0:T(8,128)(2,1)}, bf16[12,576,512]{2,1,0:T(8,128)(2,1)}) custom-call(bf16[12,4096,512]{2,1,0:T(8,128)(2,1)} %get-tuple-element.55.dgs, bf16[12,4096,512]{2,1,0:T(8,128)(2,1)} %get-tuple-element.56.dus, ...), custom_call_target="tpu_custom_call", output_to_operand_aliasing={{1}: (5, {}), {2}: (6, {})} | custom-call | flops 38654705664 | bytes 157286400 | tf_op jit(solution)/shard_map/input_pass/pallas_call | solution.py:550
  867.9 60.9 %last_pass.1 = (bf16[2,2048,768]{2,1,0:T(8,128)(2,1)}, bf16[2,192,6144]{2,1,0:T(8,128)(2,1)}, bf16[2,192,6144]{2,1,0:T(8,128)(2,1)}, bf16[2,1536,768]{2,1,0:T(8,128)(2,1)}) custom-call(bf16[12,4096,512]{2,1,0:T(8,128)(2,1)} %get-tuple-element.55.dgs, bf16[12,4096,512]{2,1,0:T(8,128)(2,1)} %get-tuple-element.56.dus, ...), custom_call_target="tpu_custom_call" | custom-call | flops 38654705664 | bytes 157286400 | tf_op jit(solution)/shard_map/last_pass/pallas_call | solution.py:608

commit v2 on v0

v2 whole, which is shorter than its diff:
```python
import functools

import jax
import jax.numpy as jnp
from jax import lax
from jax.experimental import pallas as pl
from jax.experimental.pallas import tpu as pltpu
from jax.sharding import PartitionSpec as P

f32, bf16 = jnp.float32, jnp.bfloat16
TOK, D, FF, L = 4096, 768, 6144, 2
S = 4
C = 512
J = FF // C
LAST = J - 1
W = C // S
RD, RF = D // S, FF // S
PR = 2 * RD + W * D // C
HALF = PR // 2
EARLY = 2
VM = 67043328
MESH = pl.DeviceIdType.MESH
once = pl.Buffered(1)
hbm = pl.BlockSpec(memory_space=pl.ANY)


def dot(a, b, ca=1, cb=0):
    return lax.dot_general(a, b, (((ca,), (cb,)), ((), ())), preferred_element_type=f32)


def dot_across(a, b):
    return dot(a, b, 1, 1)


def params(matmuls, mib, **more):
    return dict(
        compiler_params=pltpu.CompilerParams(vmem_limit_bytes=VM, **more),
        cost_estimate=pl.CostEstimate(flops=2 * matmuls * TOK * D * FF, bytes_accessed=mib << 20, transcendentals=0),
    )


def place_in_grid():
    return pl.program_id(0), pl.program_id(1)


def normed(wide):
    scale = lax.rsqrt(jnp.mean(wide**2, -1, keepdims=True) + 1e-6)
    return (wide * scale).astype(bf16)


def norm_back(by, h, dy):
    by, wide = by.astype(bf16).astype(f32), h.astype(f32)
    scale = lax.rsqrt(jnp.mean(wide**2, -1, keepdims=True) + 1e-6)
    along = jnp.sum(by * wide, -1, keepdims=True) / D
    by_h = (by * scale - wide * (scale * scale * scale * along)).astype(bf16)
    return (dy.astype(f32) + by_h.astype(f32)).astype(bf16)


def gate_of(w):
    return jnp.concatenate([w[s, 0:RD, :] for s in range(S)], axis=0)


def up_of(w):
    return jnp.concatenate([w[s, RD : 2 * RD, :] for s in range(S)], axis=0)


def down_of(w, at=2 * RD):
    def rows(s):
        fold = jnp.concatenate([w[s, at + W : at + W + W // 2, 0 : D - C], w[s, at + W : at + W + W // 2, D - C : 2 * (D - C)]], axis=0)
        return jnp.concatenate([w[s, at : at + W, :], fold], axis=1)

    return jnp.concatenate([rows(s) for s in range(S)], axis=0)


def piece_slices(j):
    for s in range(S):
        cols = pl.ds(pl.multiple_of(RF * s + W * j, W), W)
        yield 0, (pl.ds(0, RD), cols), (pl.ds(0, RD), pl.ds(W * s, W))
        yield 1, (pl.ds(0, RD), cols), (pl.ds(RD, RD), pl.ds(W * s, W))
    at = pl.multiple_of(W * j, W)
    yield 2, (pl.ds(at, W), pl.ds(0, C)), (pl.ds(2 * RD, W), pl.ds(0, C))
    yield 2, (pl.ds(at, W // 2), pl.ds(C, D - C)), (pl.ds(2 * RD + W, W // 2), pl.ds(0, D - C))
    yield 2, (pl.ds(at + W // 2, W // 2), pl.ds(C, D - C)), (pl.ds(2 * RD + W, W // 2), pl.ds(D - C, D - C))


def place():
    me, y = lax.axis_index("s"), lax.axis_index("r")
    return me, y, {"s": me + 1 - 2 * lax.rem(me, 2)}, {"s": lax.rem(me + 2, S)}, {"r": 1 - y}


def greet():
    _, _, core, across, copy = place()
    barrier = pltpu.get_barrier_semaphore()
    for to in (core, across, copy):
        pl.semaphore_signal(barrier, inc=1, device_id=to, device_id_type=MESH)
    pl.semaphore_wait(barrier, 3)


def remote(src, dst, send, recv, to):
    return pltpu.make_async_remote_copy(src_ref=src, dst_ref=dst, send_sem=send, recv_sem=recv, device_id=to, device_id_type=MESH)


FROM = (0, 1, 2, 0, 0)


def wait_pieces(whole, n, sem):
    ref = whole.at[0, pl.ds(0, n), 0]
    pltpu.make_async_copy(ref, ref, sem).wait()


class Gather:
    def __init__(self, first, mine, whole, stage, send, recv, local):
        self.first, self.mine, self.whole, self.stage = first, mine, whole, stage
        self.send, self.recv, self.local, self.ring = send, recv, local, stage.shape[0]

    @staticmethod
    def scratch(n, ring):
        return [
            pltpu.VMEM((ring, PR, C), bf16),
            pltpu.SemaphoreType.DMA((ring,)),
            pltpu.SemaphoreType.DMA((n, 3)),
            pltpu.SemaphoreType.DMA((ring, 2)),
        ]

    def copy(self, k, n):
        me, y, core, across, copy = place()
        l, j, slot = k // J, lax.rem(k, J), lax.rem(k, self.ring)
        near, far = pl.ds(pl.multiple_of(HALF * y, HALF), HALF), pl.ds(pl.multiple_of(HALF * (1 - y), HALF), HALF)
        rows = ((), (near,), (near,), (near,), (far,))[n]
        s = me if n < 2 else lax.rem(me + 2, S)
        what = self.whole.at[(l, s, j, *rows)]
        src = self.stage.at[(slot, *rows)] if n < 2 else what
        return remote(src, what, self.send.at[slot], self.recv.at[k - self.first, FROM[n]], (core, across, copy, core, core)[n])

    def keep(self, k):
        slot = lax.rem(k, self.ring)
        return pltpu.make_async_copy(self.stage.at[slot], self.whole.at[k // J, place()[0], lax.rem(k, J)], self.local.at[slot, 1])

    def pack(self, k):
        slot = lax.rem(k, self.ring)
        for m, src, dst in piece_slices(lax.rem(k, J)):
            pltpu.make_async_copy(self.mine[m].at[(k // J, *src)], self.stage.at[(slot, *dst)], self.local.at[slot, 0]).start()

    def start(self, k):
        slot = lax.rem(k, self.ring)
        pltpu.make_async_copy(self.stage.at[slot], self.stage.at[slot], self.local.at[slot, 0]).wait()
        self.copy(k, 1).start()
        self.copy(k, 0).start()
        self.keep(k).start()

    def across(self, k):
        self.copy(k, 1).wait_recv()
        self.copy(k, 2).start()
        self.copy(k, 3).start()

    def along(self, k):
        self.copy(k, 2).wait_recv()
        self.copy(k, 4).start()

    def finish(self, k):
        wait_pieces(self.whole, 2, self.recv.at[k - self.first, 0])
        wait_pieces(self.whole, 3, self.send.at[lax.rem(k, self.ring)])
        self.keep(k).wait()


def fetch(whole, held, sem, l, j):
    slot = lax.rem(j, 2)
    return pltpu.make_async_copy(whole.at[l, :, j], held.at[slot], sem.at[slot])


SWIFT = 2
PARTS = 3
ALL, SOON, LATE = (0, PARTS), (0, PARTS - 1), (PARTS - 1, PARTS)


class Swift(Gather):
    def __init__(self, mine, whole, held, send, recv, local):
        self.mine, self.whole, self.held, self.send, self.recv, self.local = mine, whole, held, send, recv, local

    SCRATCH = [pltpu.SemaphoreType.DMA((SWIFT,)), pltpu.SemaphoreType.DMA((SWIFT, 3, PARTS)), pltpu.SemaphoreType.DMA((SWIFT, 2))]

    def copies(self, k, n, parts=ALL):
        me, y, core, across, copy = place()
        s = me if n < 2 else lax.rem(me + 2, S)
        to = (core, across, copy, core, core)[n]
        for i in range(*parts) if n else (0,):
            rows = HALF * (1 - y if n == 4 else y) + HALF // PARTS * i
            what = self.held.at[(k, s, pl.ds(pl.multiple_of(rows, HALF // PARTS), HALF // PARTS)) if n else (k, s)]
            yield remote(what, what, self.send.at[k], self.recv.at[k, FROM[n], i if FROM[n] else 0], to)

    def keep(self, k):
        return pltpu.make_async_copy(self.held.at[k], self.whole.at[0, :, k], self.local.at[k, 1])

    def pack(self, k):
        for m, src, dst in piece_slices(k):
            pltpu.make_async_copy(self.mine[m].at[(0, *src)], self.held.at[(k, place()[0], *dst)], self.local.at[k, 0]).start()

    def start(self, k):
        own = self.held.at[k, place()[0]]
        pltpu.make_async_copy(own, own, self.local.at[k, 0]).wait()
        for n in (1, 0):
            for copy in self.copies(k, n):
                copy.start()

    def across(self, k, parts=ALL):
        for x, y, core in zip(*(self.copies(k, n, parts) for n in (1, 2, 3))):
            x.wait_recv()
            y.start()
            core.start()

    def along(self, k, parts=ALL):
        for y, core in zip(*(self.copies(k, n, parts) for n in (2, 4))):
            y.wait_recv()
            core.start()

    def finish(self, k):
        wait_pieces(self.whole, 2, self.recv.at[k, 0, 0])
        wait_pieces(self.whole, 3, self.send.at[k])
        self.keep(k).start()


def rows_of(t, T):
    return pl.ds(pl.multiple_of(t * T, T), T)


def in_turn(low, high, f):
    def body(i, _):
        f(i)
        return 0

    lax.fori_loop(low, high, body, 0)


def by_rows(low, high, f):
    n = 256
    in_turn(low // n, high // n, lambda i: f(rows_of(i, n)))


def forward_kernel(T, x_i, wg, wu, wd, h_o, a0_o, a1_o, gs, us, whole, x, a, acc, held, load, io, first, *rest):
    j, t = place_in_grid()
    swift = Swift((wg, wu, wd), whole, held, *rest[:3])
    gather = Gather(SWIFT, (wg, wu, wd), whole, *rest[3:])
    ahead, K, NT = 4, J + EARLY, TOK // T
    assert NT == 2 and SWIFT == 2 and EARLY == 2
    rows = pl.ds(pl.multiple_of(t * T, T), T)

    def outs(t):
        part = pl.ds(pl.multiple_of(t * T, T), T)
        return [pltpu.make_async_copy(x.at[part], h_o.at[part], io.at[1, t]), pltpu.make_async_copy(a.at[part], a1_o.at[part], io.at[2, t])]

    def take(j):
        fetch(whole, held, load, 0, j).start()

    @pl.when((j == 0) & (t == 0))
    def _():
        n = 4
        states = lambda i: pltpu.make_async_copy(x_i.at[rows_of(i, TOK // n)], x.at[rows_of(i, TOK // n)], first.at[i])
        swift.pack(0)
        states(0).start()
        swift.pack(1)
        for i in range(1, n):
            states(i).start()
        greet()
        for k in range(SWIFT):
            swift.start(k)
        in_turn(SWIFT, ahead + 2, gather.pack)

        def norm(i):
            states(i).wait()

            def some(rows):
                a[rows, :] = normed(x[rows, :].astype(f32))

            by_rows(TOK // n * i, TOK // n * (i + 1), some)

        norm(0)
        swift.across(0)
        gather.start(SWIFT)
        in_turn(1, n, norm)
        pltpu.make_async_copy(a, a0_o, io.at[0, 1]).start()
        swift.along(0)
        in_turn(SWIFT + 1, ahead + 1, gather.start)
        swift.across(1, SOON)
        swift.finish(0)

    @pl.when((t == 0) & (j > 0))
    def _():
        @pl.when(j == 1)
        def _():
            swift.along(1, LATE)
            swift.finish(1)

        @pl.when(j >= SWIFT)
        def _():
            fetch(whole, held, load, 0, j).wait()

            gather.along(j + 1)

        @pl.when(j < LAST)
        def _():
            gather.across(j + 2)

        @pl.when(j == LAST)
        def _():
            gather.along(J + 1)

        @pl.when(j + ahead < K)
        def _():
            gather.start(j + ahead)

        @pl.when(j + ahead + 1 < K)
        def _():
            gather.pack(j + ahead + 1)

    @pl.when(t == 1)
    def _():
        @pl.when(j == 0)
        def _():
            swift.across(1, LATE)
            swift.along(1, SOON)
            gather.across(SWIFT)

        @pl.when(j == 1)
        def _():
            gather.along(2)

        @pl.when(j > 0)
        def _():
            gather.finish(j + 1)

        @pl.when((j == 1) | (j == 2))
        def _():
            swift.keep(j - 1).wait()

        @pl.when((j > 0) & (j + 1 < J))
        def _():
            take(j + 1)

        @pl.when(j == J - 2)
        def _():
            gather.across(J + 1)

        @pl.when(j == LAST)
        def _():
            gather.finish(J + 1)

    w = held.at[lax.rem(j, 2)]
    lhs = a[rows, :]
    g, u = dot(lhs, gate_of(w)), dot(lhs, up_of(w))
    gs[0], us[0] = g, u
    act = (g * jax.nn.sigmoid(g) * u).astype(bf16)
    acc[rows, :] = jnp.where(j == 0, 0.0, acc[rows, :]) + dot(act, down_of(w))

    @pl.when(j == LAST)
    def _():
        @pl.when(t == 0)
        def _():
            pltpu.make_async_copy(a, a0_o, io.at[0, 1]).wait()

        def some(rows):
            h = (x[rows, :].astype(f32) + acc[rows, :].astype(bf16).astype(f32)).astype(bf16)
            x[rows, :] = h
            a[rows, :] = normed(h.astype(f32))

        by_rows(t * T, (t + 1) * T, some)
        for copy in outs(t):
            copy.start()

        @pl.when(t == NT - 1)
        def _():
            for i in range(NT):
                for copy in outs(i):
                    copy.wait()


def forward(x, wg, wu, wd):
    T = 2048
    tile = pl.BlockSpec((1, T, C), lambda j, t: (j, t, 0))
    states = jax.ShapeDtypeStruct((TOK, D), bf16)
    return pl.pallas_call(
        functools.partial(forward_kernel, T),
        grid=(J, TOK // T),
        in_specs=[hbm] * 4,
        out_specs=[hbm] * 3 + [tile, tile, hbm],
        out_shape=[states] * 3 + [jax.ShapeDtypeStruct((J, TOK, C), f32)] * 2 + [jax.ShapeDtypeStruct((L, S, J, PR, C), bf16)],
        scratch_shapes=[
            pltpu.VMEM((TOK, D), bf16),
            pltpu.VMEM((TOK, D), bf16),
            pltpu.VMEM((TOK, D), f32),
            pltpu.VMEM((2, S, PR, C), bf16),
            pltpu.SemaphoreType.DMA((2,)),
            pltpu.SemaphoreType.DMA((3, 2)),
            pltpu.SemaphoreType.DMA((4,)),
        ]
        + Swift.SCRATCH
        + Gather.scratch(J + EARLY - SWIFT, 6),
        **params(3, 250, collective_id=0, has_side_effects=True),
        name="forward",
    )(x, wg, wu, wd)


def pack(s, ag, au, ad):
    rows, down = pl.ds(pl.multiple_of(RD * s, RD), RD), pl.multiple_of(W * s, W)
    yield slice(0, RD), slice(0, C), ag[rows, :]
    yield slice(RD, 2 * RD), slice(0, C), au[rows, :]
    yield slice(2 * RD, 2 * RD + W), slice(0, C), ad[pl.ds(down, W), :C]
    yield slice(2 * RD + W, PR), slice(0, D - C), ad[pl.ds(down, W // 2), C:]
    yield slice(2 * RD + W, PR), slice(D - C, C), ad[pl.ds(down + W // 2, W // 2), C:]


class Reduce:
    def __init__(self, sums, theirs, kept, out_a, in_a, kept_b, out_b, in_b, out_c, sems):
        self.sums, self.theirs = sums, theirs
        self.kept, self.out_a, self.in_a = kept, out_a, in_a
        self.kept_b, self.out_b, self.in_b, self.out_c = kept_b, out_b, in_b, out_c
        self.sems = sems

    SCRATCH = [
        pltpu.VMEM((2, PR, C), f32),
        pltpu.VMEM((2, PR, C), bf16),
        pltpu.VMEM((2, 2, PR, C), bf16),
        pltpu.VMEM((PR, C), f32),
        pltpu.VMEM((PR, C), bf16),
        pltpu.VMEM((2, PR, C), bf16),
        pltpu.VMEM((PR, C), bf16),
        pltpu.SemaphoreType.DMA((3, 4)),
    ]

    def at(self, sums, theirs):
        return Reduce(sums, theirs, self.kept, self.out_a, self.in_a, self.kept_b, self.out_b, self.in_b, self.out_c, self.sems)

    def copy_a(self, j, src=None):
        slot = lax.rem(j, 2)
        return remote(self.out_a if src is None else src, self.in_a.at[slot], self.sems.at[0, 0], self.sems.at[0, 1 + slot], place()[2])

    def copy_b(self, j):
        slot = lax.rem(j, 2)
        return remote(self.out_b, self.in_b.at[slot], self.sems.at[1, 0], self.sems.at[1, 1 + slot], place()[3])

    def copy_c(self, j):
        return remote(self.out_c, self.theirs.at[j], self.sems.at[2, 0], self.sems.at[2, 1 + lax.rem(j, 2)], place()[4])

    def store_c(self, j):
        return pltpu.make_async_copy(self.out_c, self.sums.at[j], self.sems.at[2, 3])

    def again_c(self, j, send, recv):
        return remote(self.sums.at[j], self.theirs.at[j], send, recv, place()[4])

    def collect(self, ag, au, ad):
        c = lax.rem(lax.axis_index("s"), 2)
        for x in range(2):
            for r, cols, v in pack(2 * x + 1 - c, ag, au, ad):
                self.out_a[x, r, cols] = v.astype(bf16)
            for r, cols, v in pack(2 * x + c, ag, au, ad):
                self.kept[x, r, cols] = v

    def step_a(self, j):
        self.copy_a(j).wait()
        slot, x = lax.rem(j, 2), lax.axis_index("s") // 2
        self.out_b[...] = (self.kept[1 - x] + self.in_a[slot, 1 - x].astype(f32)).astype(bf16)
        self.copy_b(j).start()
        self.kept_b[...] = self.kept[x] + self.in_a[slot, x].astype(f32)

    def step_b(self, j, send=True):
        self.copy_b(j).wait()
        self.out_c[...] = (self.kept_b[...] + self.in_b[lax.rem(j, 2)].astype(f32)).astype(bf16)
        if send:
            self.copy_c(j).start()
        self.store_c(j).start()

    def step_c(self, j):
        self.copy_c(j).wait()
        self.store_c(j).wait()

    def follow(self, j):
        for stage, step in ((3, self.step_c), (2, self.step_b), (1, self.step_a)):
            pl.when(j >= stage)(functools.partial(step, j - stage))

    def handed(self, kept, out_a, sems):
        return [pltpu.make_async_copy(src, dst, sems.at[i]) for i, (src, dst) in enumerate(((self.kept, kept), (self.out_a, out_a)))]

    def leave(self, copies):
        self.step_c(J - 3)
        self.step_b(J - 2, send=False)
        self.store_c(J - 2).wait()
        for copy in copies:
            copy.wait()


def gradients(by, g, u):
    sig = jax.nn.sigmoid(g)
    silu = g * sig
    return (silu * u).astype(bf16), (by * u * (sig + silu * (1 - sig))).astype(bf16), (by * silu).astype(bf16)


def accumulate(t, a, dy, act, dg, du, ag, au, ad):
    for acc, l, r in ((ag, a, dg), (au, a, du), (ad, act, dy)):
        acc[...] = jnp.where(t == 0, 0.0, acc[...]) + dot(l, r, 0, 0)


PIECE = 512


class Pair:
    def __init__(self, *copies):
        self.copies = copies

    def start(self):
        for copy in self.copies:
            copy.start()

    def wait(self):
        for copy in self.copies:
            copy.wait()


def state_copies(i, first, second, sems):
    rows = rows_of(i, PIECE)
    return Pair(*(pltpu.make_async_copy(src.at[rows], dst.at[rows], sems.at[n, i]) for n, (src, dst) in enumerate((first, second))))


def second_kernel(a_i, dy_i, h, wg, wu, wd, _, out, sums, theirs, kept_o, out_o, whole, a, dy, ag, au, ad, total, held, load, save, states, *rest):
    j, t = place_in_grid()
    NT = 4
    T = TOK // NT
    gather = Gather(J + EARLY, (wg, wu, wd), whole, *rest[:4])
    reduce = Reduce(sums, theirs, *rest[4:])
    lead = EARLY + 1
    rows = rows_of(t, T)

    parts = T // PIECE

    def inputs(i):
        return state_copies(i, (a_i, a), (dy_i, dy), states)

    def layer_input(i):
        return pltpu.make_async_copy(h.at[rows_of(i, PIECE)], a.at[rows_of(i, PIECE)], states.at[0, i])

    def result(i):
        return pltpu.make_async_copy(dy.at[rows_of(i, PIECE)], out.at[rows_of(i, PIECE)], states.at[1, i])

    @pl.when((j == 0) & (t == 0))
    def _():
        in_turn(J + EARLY, J + lead + 1, gather.pack)
        fetch(whole, held, load, 1, 0).start()
        in_turn(0, NT * parts, lambda i: inputs(i).start())
        greet()
        gather.start(J + EARLY)

    @pl.when(j == 0)
    def _():
        in_turn(parts * t, parts * (t + 1), lambda i: inputs(i).wait())

    @pl.when(t == 0)
    def _():
        fetch(whole, held, load, 1, j).wait()

        @pl.when((j + 1 >= EARLY) & (j + 1 < J))
        def _():
            gather.along(J + j + 1)

        @pl.when(j + lead < J)
        def _():
            gather.start(J + j + lead)

        @pl.when(j + lead + 1 < J)
        def _():
            gather.pack(J + j + lead + 1)

    @pl.when(t == 1)
    def _():
        reduce.follow(j)

    @pl.when((t == 2) & (j + 2 < J))
    def _():
        gather.across(J + j + 2)

    @pl.when((t == 3) & (j + 1 < J))
    def _():
        @pl.when(j + 1 >= EARLY)
        def _():
            gather.finish(J + j + 1)

        fetch(whole, held, load, 1, j + 1).start()

    w = held.at[lax.rem(j, 2)]
    lhs, ct = a[rows, :], dy[rows, :]
    gate, up = gate_of(w), up_of(w)
    g, u = dot(lhs, gate), dot(lhs, up)
    by = dot_across(ct, down_of(w)).astype(bf16).astype(f32)
    act, dg, du = gradients(by, g, u)
    accumulate(t, lhs, ct, act, dg, du, ag, au, ad)
    total[rows, :] = jnp.where(j == 0, 0.0, total[rows, :]) + (dot_across(dg, gate) + dot_across(du, up))

    @pl.when(t == NT - 1)
    def _():
        reduce.collect(ag, au, ad)

        @pl.when(j < LAST)
        def _():
            reduce.copy_a(j).start()

    @pl.when(j == LAST)
    def _():
        in_turn(parts * t, parts * (t + 1), lambda i: layer_input(i).start())

        @pl.when(t == NT - 1)
        def _():
            copies = reduce.handed(kept_o, out_o, save)
            for copy in copies:
                copy.start()

            def back(i):
                layer_input(i).wait()

                def some(rows):
                    dy[rows, :] = norm_back(total[rows, :], a[rows, :], dy[rows, :])

                by_rows(i * PIECE, (i + 1) * PIECE, some)
                result(i).start()

            in_turn(0, NT * parts, back)
            reduce.leave(copies)
            in_turn(0, NT * parts, lambda i: result(i).wait())


PIECES = jax.ShapeDtypeStruct((J, PR, C), bf16)


def second_pass(a, dy, h, wg, wu, wd, whole):
    T = TOK // 4
    return pl.pallas_call(
        second_kernel,
        grid=(J, TOK // T),
        in_specs=[hbm] * 7,
        out_specs=[hbm] * 6,
        out_shape=[jax.ShapeDtypeStruct((TOK, D), bf16), PIECES, PIECES]
        + [jax.ShapeDtypeStruct((2, PR, C), f32), jax.ShapeDtypeStruct((2, PR, C), bf16), jax.ShapeDtypeStruct((L, S, J, PR, C), bf16)],
        scratch_shapes=[
            pltpu.VMEM((TOK, D), bf16),
            pltpu.VMEM((TOK, D), bf16),
            pltpu.VMEM((D, C), f32),
            pltpu.VMEM((D, C), f32),
            pltpu.VMEM((C, D), f32),
            pltpu.VMEM((TOK, D), f32),
            pltpu.VMEM((2, S, PR, C), bf16),
            pltpu.SemaphoreType.DMA((2,)),
            pltpu.SemaphoreType.DMA((2,)),
            pltpu.SemaphoreType.DMA((2, TOK // PIECE)),
        ]
        + Gather.scratch(J - EARLY, 4)
        + Reduce.SCRATCH,
        input_output_aliases={6: 5},
        **params(8, 100, collective_id=1, has_side_effects=True),
        name="second_pass",
    )(a, dy, h, wg, wu, wd, whole)


def first_kernel(a_i, dy_i, w, gs, us, s1_i, t1_i, kept_i, out_i, dgs, dus, sums, theirs, kept_o, out_o, s1, t1, a, dy, ag, au, ad, save, states, *rest):
    j, t = place_in_grid()
    T = dgs.shape[1]
    NT = TOK // T
    rows = rows_of(t, T)
    reduce = Reduce(sums, theirs, *rest)
    before = reduce.at(s1, t1)
    kept = lambda: pltpu.make_async_copy(kept_i, reduce.kept, save.at[0])
    again = lambda: before.again_c(J - 2, save.at[1], save.at[2])

    parts = T // PIECE

    def inputs(i):
        return state_copies(i, (a_i, a), (dy_i, dy), states)

    @pl.when((j == 0) & (t == 0))
    def _():
        in_turn(0, parts, lambda i: inputs(i).start())
        kept().start()
        in_turn(parts, NT * parts, lambda i: inputs(i).start())
        greet()
        before.copy_a(LAST, out_i).start()
        again().start()

    @pl.when(j == 0)
    def _():
        in_turn(parts * t, parts * (t + 1), lambda i: inputs(i).wait())

    @pl.when(t == 1)
    def _():
        @pl.when(j == 2)
        def _():
            before.step_c(LAST)

        @pl.when(j == 1)
        def _():
            again().wait()
            before.step_b(LAST)

        @pl.when(j == 0)
        def _():
            kept().wait()
            before.step_a(LAST)

        reduce.follow(j)

    lhs, ct = a[rows, :], dy[rows, :]
    by = dot_across(ct, down_of(w.at[0, :, 0], 0)).astype(bf16).astype(f32)
    act, dg, du = gradients(by, gs[0], us[0])
    dgs[0], dus[0] = dg, du
    accumulate(t, lhs, ct, act, dg, du, ag, au, ad)

    @pl.when(t == NT - 1)
    def _():
        reduce.collect(ag, au, ad)

        @pl.when(j < LAST)
        def _():
            reduce.copy_a(j).start()

        @pl.when(j == LAST)
        def _():
            copies = reduce.handed(kept_o, out_o, save)
            for copy in copies:
                copy.start()
            reduce.leave(copies)


def first_pass(a, dy, whole, gs, us, s1, t1, kept, out_a):
    T = 1024
    tile = pl.BlockSpec((1, T, C), lambda j, t: (j, t, 0))
    return pl.pallas_call(
        first_kernel,
        grid=(J, TOK // T),
        in_specs=[hbm, hbm, pl.BlockSpec((1, S, 1, PR - 2 * RD, C), lambda j, t: (0, 0, j, 2, 0)), tile, tile] + [hbm] * 4,
        out_specs=[tile, tile] + [hbm] * 6,
        out_shape=[jax.ShapeDtypeStruct((J, TOK, C), bf16)] * 2
        + [PIECES, PIECES, jax.ShapeDtypeStruct((2, PR, C), f32), jax.ShapeDtypeStruct((2, PR, C), bf16), PIECES, PIECES],
        scratch_shapes=[
            pltpu.VMEM((TOK, D), bf16),
            pltpu.VMEM((TOK, D), bf16),
            pltpu.VMEM((D, C), f32),
            pltpu.VMEM((D, C), f32),
            pltpu.VMEM((C, D), f32),
            pltpu.SemaphoreType.DMA((3,)),
            pltpu.SemaphoreType.DMA((2, TOK // PIECE)),
        ]
        + Reduce.SCRATCH,
        input_output_aliases={5: 6, 6: 7},
        **params(4, 300, collective_id=2, has_side_effects=True),
        name="first_pass",
    )(a, dy, whole, gs, us, s1, t1, kept, out_a)


PART = TOK // 2


Q = 2
STEPS = J // Q
END = STEPS - 1


def contract(j, dgs, dus, w, acc):
    n = PART // Q
    for i in range(PART // n):
        rows = slice(i * n, (i + 1) * n)
        total = jnp.where(j == 0, 0.0, acc[rows, :])
        for q in range(Q):
            held = w.at[0, :, q]
            total = total + (dot_across(dgs[q, rows], gate_of(held)) + dot_across(dus[q, rows], up_of(held)))
        acc[rows, :] = total


def input_kernel(dgs, dus, w, h_i, dy_i, s1, t1, s_i, t_i, kept_i, out_i, g1, out, sums, theirs, acc, h, dy, save, states, *rest):
    reduce = Reduce(sums, theirs, *rest)
    j = pl.program_id(0)
    late_states(0, j, h_i, dy_i, h, dy, states)

    @pl.when(j == 0)
    def _():
        pltpu.make_async_copy(kept_i, reduce.kept, save.at[0]).start()
        greet()
        reduce.copy_a(LAST, out_i).start()
        reduce.again_c(J - 2, save.at[1], save.at[2]).start()

    @pl.when(j == 1)
    def _():
        pltpu.make_async_copy(kept_i, reduce.kept, save.at[0]).wait()
        reduce.step_a(LAST)

    @pl.when(j == 3)
    def _():
        reduce.step_b(LAST)

    @pl.when(j == END)
    def _():
        reduce.again_c(J - 2, save.at[1], save.at[2]).wait()
        reduce.step_c(LAST)

    g1[...] = (s1[...].astype(f32) + t1[...].astype(f32)).astype(bf16)
    contract(j, dgs, dus, w, acc)

    @pl.when(j == END)
    def _():
        def some(rows):
            out[rows, :] = norm_back(acc[rows, :], h[rows, :], dy[rows, :])

        by_rows(0, PART, some)


def late_states(part, j, h_i, dy_i, h, dy, sems):
    copies = lambda: [pltpu.make_async_copy(src.at[pl.ds(part * PART, PART)], dst, sems.at[i]) for i, (src, dst) in enumerate(((h_i, h), (dy_i, dy)))]

    @pl.when(j == 2)
    def _():
        for copy in copies():
            copy.start()

    @pl.when(j == END)
    def _():
        for copy in copies():
            copy.wait()


STATES = [pltpu.VMEM((PART, D), f32), pltpu.VMEM((PART, D), bf16), pltpu.VMEM((PART, D), bf16)]
piece = pl.BlockSpec((Q, PR, C), lambda j: (j, 0, 0))


def part_specs(part):
    tile = pl.BlockSpec((Q, PART, C), lambda j: (j, part, 0))
    return [tile, tile, pl.BlockSpec((1, S, Q, 2 * RD, C), lambda j: (0, 0, j, 0, 0)), hbm, hbm]


def input_pass(dgs, dus, whole, h, dy, s1, t1, sums, theirs, kept, out_a):
    return pl.pallas_call(
        input_kernel,
        grid=(STEPS,),
        in_specs=part_specs(0) + [piece, piece] + [hbm] * 4,
        out_specs=[piece, pl.BlockSpec((PART, D), lambda j: (0, 0), pipeline_mode=once), hbm, hbm],
        out_shape=[PIECES, jax.ShapeDtypeStruct((PART, D), bf16), PIECES, PIECES],
        scratch_shapes=STATES + [pltpu.SemaphoreType.DMA((3,)), pltpu.SemaphoreType.DMA((2,))] + Reduce.SCRATCH,
        input_output_aliases={7: 2, 8: 3},
        **params(1, 100, collective_id=3, has_side_effects=True),
        name="input_pass",
    )(dgs, dus, whole, h, dy, s1, t1, sums, theirs, kept, out_a)


def last_kernel(dgs, dus, w, h_i, dy_i, g1, s0, t0, begun, out, og, ou, od, acc, h, dy, stage, passing, sems, io, states):
    j = pl.program_id(0)
    late_states(1, j, h_i, dy_i, h, dy, states)
    slot = lax.rem(j, 2)
    first = lambda: pltpu.make_async_copy(begun, passing, io.at[0])
    second = lambda: pltpu.make_async_copy(passing, out.at[0], io.at[1])

    def wait(slot):
        for l in range(L):
            pltpu.make_async_copy(stage.at[slot, l], stage.at[slot, l], sems.at[slot, l]).wait()

    @pl.when(j == 0)
    def _():
        first().start()

    @pl.when(j == 2)
    def _():
        first().wait()
        second().start()

    @pl.when(j >= 2)
    def _():
        wait(slot)

    stage[slot, 0] = (s0[...].astype(f32) + t0[...].astype(f32)).astype(bf16)
    stage[slot, 1] = g1[...]
    contract(j, dgs, dus, w, acc)
    for l in range(L):

        def unpack(q):
            for m, dst, src in piece_slices(Q * j + q):
                pltpu.make_async_copy(stage.at[(slot, l, q, *src)], (og, ou, od)[m].at[(l, *dst)], sems.at[slot, l]).start()

        in_turn(0, Q, unpack)

    @pl.when(j == END)
    def _():
        n = 4
        result = lambda i: pltpu.make_async_copy(dy.at[rows_of(i, PART // n)], out.at[1, rows_of(i, PART // n)], io.at[2 + i])

        def quarter(i):
            def some(rows):
                dy[rows, :] = norm_back(acc[rows, :], h[rows, :], dy[rows, :])

            by_rows(PART // n * i, PART // n * (i + 1), some)
            result(i).start()

        in_turn(0, n, quarter)
        wait(1 - slot)
        wait(slot)
        second().wait()
        in_turn(0, n, lambda i: result(i).wait())


def last_pass(dgs, dus, whole, h, dy, g1, s0, t0, begun):
    return pl.pallas_call(
        last_kernel,
        grid=(STEPS,),
        in_specs=part_specs(1) + [piece] * 3 + [hbm],
        out_specs=[hbm] * 4,
        out_shape=[jax.ShapeDtypeStruct((2, PART, D), bf16)] + [jax.ShapeDtypeStruct((L, RD, FF), bf16)] * 2 + [jax.ShapeDtypeStruct((L, RF, D), bf16)],
        scratch_shapes=STATES
        + [
            pltpu.VMEM((2, L, Q, PR, C), bf16),
            pltpu.VMEM((PART, D), bf16),
            pltpu.SemaphoreType.DMA((2, L)),
            pltpu.SemaphoreType.DMA((6,)),
            pltpu.SemaphoreType.DMA((2,)),
        ],
        **params(1, 150),
        name="last_pass",
    )(dgs, dus, whole, h, dy, g1, s0, t0, begun)


def solution(mesh):
    def step(x, dy, *weights):
        x, dy = x[0], dy[0]
        h1, a0, a1, gs, us, whole = forward(x, *weights)
        by1, s1, t1, kept, out_a, whole = second_pass(a1, dy, h1, *weights, whole)
        dgs, dus, s0, t0, kept, out_a, s1, t1 = first_pass(a0, by1, whole, gs, us, s1, t1, kept, out_a)
        g1, begun, s0, t0 = input_pass(dgs, dus, whole, x, by1, s1, t1, s0, t0, kept, out_a)
        by0, *grads = last_pass(dgs, dus, whole, x, by1, g1, s0, t0, begun)
        return (by0.reshape(1, TOK, D), *grads)

    states, cut = P(("rep", "r", "s"), None, None), P(None, "s", None)
    return jax.shard_map(
        step,
        mesh=mesh,
        in_specs=(states, states) + (cut,) * 3,
        out_specs=(states,) + (P("rep", "s", None),) * 3,
        check_vma=False,
    )
```

time: 1590 us -> 828 us (0.52)
  matrix products: 1100 us -> 0 us
  Pallas kernels: 0 us -> 827 us
  waiting for transfers between devices: 383 us -> 0 us
  local copies, waits for them, and re-layouts: 44.2 us -> 0 us
  other arithmetic: 36.8 us -> 0 us
    dot_general x17 -> x0, matrix products: 1100 us -> none  [the longest x6 402 us: layer(): up = jnp.dot(a, w['w_up'], preferred_element_type=jnp.float32)]
    pallas_call x0 -> x5, Pallas kernels: none -> 827 us  [the longest x1 356 us: second_pass(): pl.pallas_call(second_kernel, grid=(J, TOK // T), in_specs=[hbm] * 7, out...]
    psum x1 -> x0, waiting for transfers between devices: 231 us -> none  [summed(): lax.psum(lax.psum_scatter(term, 's', scatter_dimension=0, tiled=True), 'r')]
    reduce_scatter x6 -> x0, waiting for transfers between devices: 93.9 us -> none  [summed(): lax.psum_scatter(term, 's', scatter_dimension=0, tiled=True)]
    all_gather x6 -> x0, waiting for transfers between devices: 56.2 us -> none  [fetched(): lax.all_gather(w[number], 's', axis=0, tiled=True)]
    unnamed x27 -> x0, local copies, waits for them, and re-layouts: 29.2 us -> none
  transfers between devices with their start and end apart: 13 -> 0, of which waited for: 6 -> 0; matrix products, arithmetic and copies ran while one was open for 55% -> 0% of each run, Pallas kernels for 0% -> 0%
where the time goes in v2:
time: 828 us
  Pallas kernels  827 us (100%)
    pallas_call x1, Pallas kernels, second_pass(): pl.pallas_call(second_kernel, grid=(J, TOK // T), in_specs=[hbm] * 7, out...  356 us
    pallas_call x1, Pallas kernels, first_pass(): pl.pallas_call(first_kernel, grid=(J, TOK // T), in_specs=[hbm, hbm, pl.B...  195 us
    pallas_call x1, Pallas kernels, forward(): pl.pallas_call(functools.partial(forward_kernel, T), grid=(J, TOK // T),...  167 us
    pallas_call x1, Pallas kernels, input_pass(): pl.pallas_call(input_kernel, grid=(STEPS,), in_specs=part_specs(0) + [pie...  55.3 us
    pallas_call x1, Pallas kernels, last_pass(): pl.pallas_call(last_kernel, grid=(STEPS,), in_specs=part_specs(1) + [piec...  54.1 us

profile of v2, /device:TPU:0, one launch (start us, length us, event | category | flops | bytes accessed | tf_op | source)
XLA Modules:
  0.0 828.3 jit_solution(18081237617064400304)
XLA Ops:
  0.6 167.2 %forward.1 = (bf16[4096,768]{1,0:T(8,128)(2,1)}, bf16[4096,768]{1,0:T(8,128)(2,1)}, bf16[4096,768]{1,0:T(8,128)(2,1)}, f32[12,4096,512]{2,1,0:T(8,128)}, f32[12,...) custom-call(bf16[4096,768]{1,0:T(8,128)(2,1)} %bitcast.3, bf16[2,192,6144]{2,1,0:T(8,128)(2,1)} %wg.3, ...), custom_call_target="tpu_custom_call" | custom-call | flops 115964116992 | bytes 262144000 | tf_op jit(solution)/shard_map/forward/pallas_call | solution.py:380
  167.8 356.3 %second_pass.1 = (bf16[4096,768]{1,0:T(8,128)(2,1)}, bf16[12,576,512]{2,1,0:T(8,128)(2,1)}, bf16[12,576,512]{2,1,0:T(8,128)(2,1)}, f32[2,576,512]{2,1,0:T(8,128)...) custom-call(bf16[4096,768]{1,0:T(8,128)(2,1)} %get-tuple-element.33.a_i, ...), custom_call_target="tpu_custom_call", output_to_operand_aliasing={{5}: (6, {})} | custom-call | flops 309237645312 | bytes 104857600 | tf_op jit(solution)/shard_map/second_pass/pallas_call | solution.py:632
  524.2 194.5 %first_pass.1 = (bf16[12,4096,512]{2,1,0:T(8,128)(2,1)}, bf16[12,4096,512]{2,1,0:T(8,128)(2,1)}, bf16[12,576,512]{2,1,0:T(8,128)(2,1)}, bf16[12,576,512]{2,1,0:T...) custom-call(bf16[4096,768]{1,0:T(8,128)(2,1)} %get-tuple-element.32., ...), custom_call_target="tpu_custom_call", output_to_operand_aliasing={{6}: (5, {}), {7}: (6, {})} | custom-call | flops 154618822656 | bytes 314572800 | tf_op jit(solution)/shard_map/first_pass/pallas_call | solution.py:730
  718.7 55.3 %input_pass.1 = (bf16[12,576,512]{2,1,0:T(8,128)(2,1)}, bf16[2048,768]{1,0:T(8,128)(2,1)}, bf16[12,576,512]{2,1,0:T(8,128)(2,1)}, bf16[12,576,512]{2,1,0:T(8,128)(2,1)}) custom-call(bf16[12,4096,512]{2,1,0:T(8,128)(2,1)} %get-tuple-element.44.dgs, bf16[12,4096,512]{2,1,0:T(8,128)(2,1)} %get-tuple-element.45.dus, ...), custom_call_target="tpu_custom_call", output_to_operand_aliasing={{2}: (7, {}), {3}: (8, {})} | custom-call | flops 38654705664 | bytes 104857600 | tf_op jit(solution)/shard_map/input_pass/pallas_call | solution.py:833
  774.0 54.1 %last_pass.1 = (bf16[2,2048,768]{2,1,0:T(8,128)(2,1)}, bf16[2,192,6144]{2,1,0:T(8,128)(2,1)}, bf16[2,192,6144]{2,1,0:T(8,128)(2,1)}, bf16[2,1536,768]{2,1,0:T(8,128)(2,1)}) custom-call(bf16[12,4096,512]{2,1,0:T(8,128)(2,1)} %get-tuple-element.44.dgs, bf16[12,4096,512]{2,1,0:T(8,128)(2,1)} %get-tuple-element.45.dus, ...), custom_call_target="tpu_custom_call" | custom-call | flops 38654705664 | bytes 157286400 | tf_op jit(solution)/shard_map/last_pass/pallas_call | solution.py:901

commit v3 on v2

--- a/solution.py
+++ b/solution.py
@@ -17,6 +17,7 @@
 RD, RF = D // S, FF // S
 PR = 2 * RD + W * D // C
 HALF = PR // 2
+BLOCKS = 2
 EARLY = 2
 VM = 67043328
 MESH = pl.DeviceIdType.MESH
@@ -236,7 +237,7 @@
     in_turn(low // n, high // n, lambda i: f(rows_of(i, n)))
 
 
-def forward_kernel(T, x_i, wg, wu, wd, h_o, a0_o, a1_o, gs, us, whole, x, a, acc, held, load, io, first, *rest):
+def forward_kernel(T, x_i, wg, wu, wd, h_o, a0_o, a1_o, saved, whole, x, a, acc, held, load, io, first, *rest):
     j, t = place_in_grid()
     swift = Swift((wg, wu, wd), whole, held, *rest[:3])
     gather = Gather(SWIFT, (wg, wu, wd), whole, *rest[3:])
@@ -345,11 +346,14 @@
             gather.finish(J + 1)
 
     w = held.at[lax.rem(j, 2)]
-    lhs = a[rows, :]
-    g, u = dot(lhs, gate_of(w)), dot(lhs, up_of(w))
-    gs[0], us[0] = g, u
-    act = (g * jax.nn.sigmoid(g) * u).astype(bf16)
-    acc[rows, :] = jnp.where(j == 0, 0.0, acc[rows, :]) + dot(act, down_of(w))
+    n = T // BLOCKS
+    for i in range(BLOCKS):
+        part, rows = slice(i * n, (i + 1) * n), rows_of(BLOCKS * t + i, n)
+        lhs = a[rows, :]
+        g, u = dot(lhs, gate_of(w)), dot(lhs, up_of(w))
+        saved[0, 0, part], saved[0, 1, part] = g, u
+        act = (g * jax.nn.sigmoid(g) * u).astype(bf16)
+        acc[rows, :] = jnp.where(j == 0, 0.0, acc[rows, :]) + dot(act, down_of(w))
 
     @pl.when(j == LAST)
     def _():
@@ -375,14 +379,14 @@
 
 def forward(x, wg, wu, wd):
     T = 2048
-    tile = pl.BlockSpec((1, T, C), lambda j, t: (j, t, 0))
+    tile = pl.BlockSpec((1, 2, T, C), lambda j, t: (j, 0, t, 0))
     states = jax.ShapeDtypeStruct((TOK, D), bf16)
     return pl.pallas_call(
         functools.partial(forward_kernel, T),
         grid=(J, TOK // T),
         in_specs=[hbm] * 4,
-        out_specs=[hbm] * 3 + [tile, tile, hbm],
-        out_shape=[states] * 3 + [jax.ShapeDtypeStruct((J, TOK, C), f32)] * 2 + [jax.ShapeDtypeStruct((L, S, J, PR, C), bf16)],
+        out_specs=[hbm] * 3 + [tile, hbm],
+        out_shape=[states] * 3 + [jax.ShapeDtypeStruct((J, 2, TOK, C), f32)] + [jax.ShapeDtypeStruct((L, S, J, PR, C), bf16)],
         scratch_shapes=[
             pltpu.VMEM((TOK, D), bf16),
             pltpu.VMEM((TOK, D), bf16),
@@ -494,8 +498,9 @@
 
 
 def accumulate(t, a, dy, act, dg, du, ag, au, ad):
-    for acc, l, r in ((ag, a, dg), (au, a, du), (ad, act, dy)):
-        acc[...] = jnp.where(t == 0, 0.0, acc[...]) + dot(l, r, 0, 0)
+    both = dot(a, jnp.concatenate([dg, du], axis=1), 0, 0)
+    for acc, term in ((ag, both[:, :C]), (au, both[:, C:]), (ad, dot(act, dy, 0, 0))):
+        acc[...] = jnp.where(t == 0, 0.0, acc[...]) + term
 
 
 PIECE = 512
@@ -656,9 +661,9 @@
     )(a, dy, h, wg, wu, wd, whole)
 
 
-def first_kernel(a_i, dy_i, w, gs, us, s1_i, t1_i, kept_i, out_i, dgs, dus, sums, theirs, kept_o, out_o, s1, t1, a, dy, ag, au, ad, save, states, *rest):
+def first_kernel(a_i, dy_i, w, gu, s1_i, t1_i, kept_i, out_i, cts, sums, theirs, kept_o, out_o, s1, t1, a, dy, ag, au, ad, save, states, *rest):
     j, t = place_in_grid()
-    T = dgs.shape[1]
+    T = cts.shape[2]
     NT = TOK // T
     rows = rows_of(t, T)
     reduce = Reduce(sums, theirs, *rest)
@@ -704,8 +709,8 @@
 
     lhs, ct = a[rows, :], dy[rows, :]
     by = dot_across(ct, down_of(w.at[0, :, 0], 0)).astype(bf16).astype(f32)
-    act, dg, du = gradients(by, gs[0], us[0])
-    dgs[0], dus[0] = dg, du
+    act, dg, du = gradients(by, gu[0, 0], gu[0, 1])
+    cts[0, 0], cts[0, 1] = dg, du
     accumulate(t, lhs, ct, act, dg, du, ag, au, ad)
 
     @pl.when(t == NT - 1)
@@ -724,15 +729,15 @@
             reduce.leave(copies)
 
 
-def first_pass(a, dy, whole, gs, us, s1, t1, kept, out_a):
+def first_pass(a, dy, whole, gu, s1, t1, kept, out_a):
     T = 1024
-    tile = pl.BlockSpec((1, T, C), lambda j, t: (j, t, 0))
+    tile = pl.BlockSpec((1, 2, T, C), lambda j, t: (j, 0, t, 0))
     return pl.pallas_call(
         first_kernel,
         grid=(J, TOK // T),
-        in_specs=[hbm, hbm, pl.BlockSpec((1, S, 1, PR - 2 * RD, C), lambda j, t: (0, 0, j, 2, 0)), tile, tile] + [hbm] * 4,
-        out_specs=[tile, tile] + [hbm] * 6,
-        out_shape=[jax.ShapeDtypeStruct((J, TOK, C), bf16)] * 2
+        in_specs=[hbm, hbm, pl.BlockSpec((1, S, 1, PR - 2 * RD, C), lambda j, t: (0, 0, j, 2, 0)), tile] + [hbm] * 4,
+        out_specs=[tile] + [hbm] * 6,
+        out_shape=[jax.ShapeDtypeStruct((J, 2, TOK, C), bf16)]
         + [PIECES, PIECES, jax.ShapeDtypeStruct((2, PR, C), f32), jax.ShapeDtypeStruct((2, PR, C), bf16), PIECES, PIECES],
         scratch_shapes=[
             pltpu.VMEM((TOK, D), bf16),
@@ -744,10 +749,10 @@
             pltpu.SemaphoreType.DMA((2, TOK // PIECE)),
         ]
         + Reduce.SCRATCH,
-        input_output_aliases={5: 6, 6: 7},
+        input_output_aliases={4: 5, 5: 6},
         **params(4, 300, collective_id=2, has_side_effects=True),
         name="first_pass",
-    )(a, dy, whole, gs, us, s1, t1, kept, out_a)
+    )(a, dy, whole, gu, s1, t1, kept, out_a)
 
 
 PART = TOK // 2
@@ -758,18 +763,18 @@
 END = STEPS - 1
 
 
-def contract(j, dgs, dus, w, acc):
+def contract(j, cts, w, acc):
     n = PART // Q
     for i in range(PART // n):
         rows = slice(i * n, (i + 1) * n)
         total = jnp.where(j == 0, 0.0, acc[rows, :])
         for q in range(Q):
             held = w.at[0, :, q]
-            total = total + (dot_across(dgs[q, rows], gate_of(held)) + dot_across(dus[q, rows], up_of(held)))
+            total = total + (dot_across(cts[q, 0, rows], gate_of(held)) + dot_across(cts[q, 1, rows], up_of(held)))
         acc[rows, :] = total
 
 
-def input_kernel(dgs, dus, w, h_i, dy_i, s1, t1, s_i, t_i, kept_i, out_i, g1, out, sums, theirs, acc, h, dy, save, states, *rest):
+def input_kernel(cts, w, h_i, dy_i, s1, t1, s_i, t_i, kept_i, out_i, g1, out, sums, theirs, acc, h, dy, save, states, *rest):
     reduce = Reduce(sums, theirs, *rest)
     j = pl.program_id(0)
     late_states(0, j, h_i, dy_i, h, dy, states)
@@ -796,7 +801,7 @@
         reduce.step_c(LAST)
 
     g1[...] = (s1[...].astype(f32) + t1[...].astype(f32)).astype(bf16)
-    contract(j, dgs, dus, w, acc)
+    contract(j, cts, w, acc)
 
     @pl.when(j == END)
     def _():
@@ -825,11 +830,10 @@
 
 
 def part_specs(part):
-    tile = pl.BlockSpec((Q, PART, C), lambda j: (j, part, 0))
-    return [tile, tile, pl.BlockSpec((1, S, Q, 2 * RD, C), lambda j: (0, 0, j, 0, 0)), hbm, hbm]
-
-
-def input_pass(dgs, dus, whole, h, dy, s1, t1, sums, theirs, kept, out_a):
+    return [pl.BlockSpec((Q, 2, PART, C), lambda j: (j, 0, part, 0)), pl.BlockSpec((1, S, Q, 2 * RD, C), lambda j: (0, 0, j, 0, 0)), hbm, hbm]
+
+
+def input_pass(cts, whole, h, dy, s1, t1, sums, theirs, kept, out_a):
     return pl.pallas_call(
         input_kernel,
         grid=(STEPS,),
@@ -837,13 +841,13 @@
         out_specs=[piece, pl.BlockSpec((PART, D), lambda j: (0, 0), pipeline_mode=once), hbm, hbm],
         out_shape=[PIECES, jax.ShapeDtypeStruct((PART, D), bf16), PIECES, PIECES],
         scratch_shapes=STATES + [pltpu.SemaphoreType.DMA((3,)), pltpu.SemaphoreType.DMA((2,))] + Reduce.SCRATCH,
-        input_output_aliases={7: 2, 8: 3},
+        input_output_aliases={6: 2, 7: 3},
         **params(1, 100, collective_id=3, has_side_effects=True),
         name="input_pass",
-    )(dgs, dus, whole, h, dy, s1, t1, sums, theirs, kept, out_a)
-
-
-def last_kernel(dgs, dus, w, h_i, dy_i, g1, s0, t0, begun, out, og, ou, od, acc, h, dy, stage, passing, sems, io, states):
+    )(cts, whole, h, dy, s1, t1, sums, theirs, kept, out_a)
+
+
+def last_kernel(cts, w, h_i, dy_i, g1, s0, t0, begun, out, og, ou, od, acc, h, dy, stage, passing, sems, io, states):
     j = pl.program_id(0)
     late_states(1, j, h_i, dy_i, h, dy, states)
     slot = lax.rem(j, 2)
@@ -869,7 +873,7 @@
 
     stage[slot, 0] = (s0[...].astype(f32) + t0[...].astype(f32)).astype(bf16)
     stage[slot, 1] = g1[...]
-    contract(j, dgs, dus, w, acc)
+    contract(j, cts, w, acc)
     for l in range(L):
 
         def unpack(q):
@@ -897,7 +901,7 @@
         in_turn(0, n, lambda i: result(i).wait())
 
 
-def last_pass(dgs, dus, whole, h, dy, g1, s0, t0, begun):
+def last_pass(cts, whole, h, dy, g1, s0, t0, begun):
     return pl.pallas_call(
         last_kernel,
         grid=(STEPS,),
@@ -914,17 +918,17 @@
         ],
         **params(1, 150),
         name="last_pass",
-    )(dgs, dus, whole, h, dy, g1, s0, t0, begun)
+    )(cts, whole, h, dy, g1, s0, t0, begun)
 
 
 def solution(mesh):
     def step(x, dy, *weights):
         x, dy = x[0], dy[0]
-        h1, a0, a1, gs, us, whole = forward(x, *weights)
+        h1, a0, a1, gu, whole = forward(x, *weights)
         by1, s1, t1, kept, out_a, whole = second_pass(a1, dy, h1, *weights, whole)
-        dgs, dus, s0, t0, kept, out_a, s1, t1 = first_pass(a0, by1, whole, gs, us, s1, t1, kept, out_a)
-        g1, begun, s0, t0 = input_pass(dgs, dus, whole, x, by1, s1, t1, s0, t0, kept, out_a)
-        by0, *grads = last_pass(dgs, dus, whole, x, by1, g1, s0, t0, begun)
+        cts, s0, t0, kept, out_a, s1, t1 = first_pass(a0, by1, whole, gu, s1, t1, kept, out_a)
+        g1, begun, s0, t0 = input_pass(cts, whole, x, by1, s1, t1, s0, t0, kept, out_a)
+        by0, *grads = last_pass(cts, whole, x, by1, g1, s0, t0, begun)
         return (by0.reshape(1, TOK, D), *grads)
 
     states, cut = P(("rep", "r", "s"), None, None), P(None, "s", None)

time: 828 us -> 827 us (level)
  no operation moved by 1% of the time
where the time goes in v3:
time: 827 us
  Pallas kernels  826 us (100%)
    pallas_call x1, Pallas kernels, second_pass(): pl.pallas_call(second_kernel, grid=(J, TOK // T), in_specs=[hbm] * 7, out...  356 us
    pallas_call x1, Pallas kernels, first_pass(): pl.pallas_call(first_kernel, grid=(J, TOK // T), in_specs=[hbm, hbm, pl.B...  195 us
    pallas_call x1, Pallas kernels, forward(): pl.pallas_call(functools.partial(forward_kernel, T), grid=(J, TOK // T),...  166 us
    pallas_call x1, Pallas kernels, input_pass(): pl.pallas_call(input_kernel, grid=(STEPS,), in_specs=part_specs(0) + [pie...  55.1 us
    pallas_call x1, Pallas kernels, last_pass(): pl.pallas_call(last_kernel, grid=(STEPS,), in_specs=part_specs(1) + [piec...  54 us

profile of v3, /device:TPU:0, one launch (start us, length us, event | category | flops | bytes accessed | tf_op | source)
XLA Modules:
  0.0 826.7 jit_solution(9672805300125050181)
XLA Ops:
  0.6 165.9 %forward.1 = (bf16[4096,768]{1,0:T(8,128)(2,1)}, bf16[4096,768]{1,0:T(8,128)(2,1)}, bf16[4096,768]{1,0:T(8,128)(2,1)}, f32[12,2,4096,512]{3,2,1,0:T(8,128)}, bf16[2,4,12,576,512]{4,3,2,1,0:T(8,128)(2,1)}) custom-call(bf16[4096,768]{1,0:T(8,128)(2,1)} %bitcast.3, bf16[2,192,6144]{2,1,0:T(8,128)(2,1)} %wg.3, bf16[2,192,6144]{2,1,0:T(8,128)(2,1)} %wu.3, ...), custom_call_target="tpu_custom_call" | custom-call | flops 115964116992 | bytes 262144000 | tf_op jit(solution)/shard_map/forward/pallas_call | solution.py:384
  166.5 356.3 %second_pass.1 = (bf16[4096,768]{1,0:T(8,128)(2,1)}, bf16[12,576,512]{2,1,0:T(8,128)(2,1)}, bf16[12,576,512]{2,1,0:T(8,128)(2,1)}, f32[2,576,512]{2,1,0:T(8,128)...) custom-call(bf16[4096,768]{1,0:T(8,128)(2,1)} %get-tuple-element.31.a_i, ...), custom_call_target="tpu_custom_call", output_to_operand_aliasing={{5}: (6, {})} | custom-call | flops 309237645312 | bytes 104857600 | tf_op jit(solution)/shard_map/second_pass/pallas_call | solution.py:637
  522.9 194.6 %first_pass.1 = (bf16[12,2,4096,512]{3,2,1,0:T(8,128)(2,1)}, bf16[12,576,512]{2,1,0:T(8,128)(2,1)}, bf16[12,576,512]{2,1,0:T(8,128)(2,1)}, f32[2,576,512]{2,1,0:...) custom-call(bf16[4096,768]{1,0:T(8,128)(2,1)} %get-tuple-element.30., ...), custom_call_target="tpu_custom_call", output_to_operand_aliasing={{5}: (4, {}), {6}: (5, {})} | custom-call | flops 154618822656 | bytes 314572800 | tf_op jit(solution)/shard_map/first_pass/pallas_call | solution.py:735
  717.4 55.1 %input_pass.1 = (bf16[12,576,512]{2,1,0:T(8,128)(2,1)}, bf16[2048,768]{1,0:T(8,128)(2,1)}, bf16[12,576,512]{2,1,0:T(8,128)(2,1)}, bf16[12,576,512]{2,1,0:T(8,128)(2,1)}) custom-call(bf16[12,2,4096,512]{3,2,1,0:T(8,128)(2,1)} %get-tuple-element.41.cts, ...), custom_call_target="tpu_custom_call", output_to_operand_aliasing={{2}: (6, {}), {3}: (7, {})} | custom-call | flops 38654705664 | bytes 104857600 | tf_op jit(solution)/shard_map/input_pass/pallas_call | solution.py:837
  772.6 54.0 %last_pass.1 = (bf16[2,2048,768]{2,1,0:T(8,128)(2,1)}, bf16[2,192,6144]{2,1,0:T(8,128)(2,1)}, bf16[2,192,6144]{2,1,0:T(8,128)(2,1)}, bf16[2,1536,768]{2,1,0:T(8,128)(2,1)}) custom-call(bf16[12,2,4096,512]{3,2,1,0:T(8,128)(2,1)} %get-tuple-element.41.cts, bf16[2,4,12,576,512]{4,3,2,1,0:T(8,128)(2,1)} %get-tuple-element.35.w, bf16[4096,768]{1,0:T(8,128)(2,1)} %bitcast.5, ...), custom_call_target="tpu_custom_call" | custom-call | flops 38654705664 | bytes 157286400 | tf_op jit(solution)/shard_map/last_pass/pallas_call | solution.py:905
